TPU v7x, 8 devices: a whole 2x2x1 slice. The times are simulated.
8 devices in a mesh: part: 1 (over z), row: 2 (over y), col: 2 (over x), dep: 2 (over core).
Axes of the slice: x: 2, y: 2, z: 1, core: 2. Of those that a mesh axis runs over, the one named last changes fastest.
Arguments:
- x_in: bfloat16 [4096, 2560], P(('part', 'row', 'col'), 'dep')
- ln_scale: float32 [2560], P('dep')
- ln_shift: float32 [2560], P('dep')
- w_up: bfloat16 [2560, 10240], P(('dep', 'row'), 'col')
- b_up: bfloat16 [10240], P('col')
- w_down: bfloat16 [10240, 2560], P(('col', 'row'), 'dep')
- b_down: bfloat16 [2560], P('dep')
- y_grad: bfloat16 [4096, 2560], P(('part', 'row', 'col'), 'dep')
Outputs:
- output 1: bfloat16 [4096, 2560], P(('part', 'row', 'col'), 'dep')
- output 2: bfloat16 [4096, 2560], P(('part', 'row', 'col'), 'dep')
- output 3: bfloat16 [2560, 10240], P(('part', 'dep', 'row'), 'col')
- output 4: float32 [10240], P(('part', 'col'))
- output 5: bfloat16 [10240, 2560], P(('part', 'col', 'row'), 'dep')
- output 6: float32 [2560], P(('part', 'dep'))
- output 7: float32 [2560], P(('part', 'dep'))
- output 8: float32 [2560], P(('part', 'dep'))
All inputs are finite; a program needn't handle non-finite values.
Results may differ from a plain program's by a relative error of at most 0.00149.
Values are sent between devices in bfloat16 or wider.
A program may use at most 1 GiB of HBM per device.

v0:
```python
import jax
import jax.numpy as jnp
from jax import lax
from jax.sharding import PartitionSpec as P

LN_EPS = 1e-5
GELU_K = 0.7978845608028654
GELU_C = 0.044715


def gelu_tanh(pre_act):
    inner_arg = GELU_K * (pre_act + GELU_C * pre_act * (pre_act * pre_act))
    return 0.5 * pre_act * (1.0 + jnp.tanh(inner_arg))


def gelu_slope(pre_act):
    squared = pre_act * pre_act
    tanh_val = jnp.tanh(GELU_K * (pre_act + GELU_C * pre_act * squared))
    return 0.5 * (1.0 + tanh_val) + 0.5 * pre_act * (1.0 - tanh_val * tanh_val) * GELU_K * (1.0 + 3.0 * GELU_C * squared)


def solution(mesh):
    dep_size = mesh.shape["dep"]
    tok_spec = P(("part", "row", "col"), "dep")
    vec_dep = P("dep")
    part_dep = P(("part", "dep"))
    in_specs = (tok_spec, vec_dep, vec_dep, P(("dep", "row"), "col"), P("col"), P(("col", "row"), "dep"), vec_dep, tok_spec)
    out_specs = (tok_spec, tok_spec, P(("part", "dep", "row"), "col"), P(("part", "col")), P(("part", "col", "row"), "dep"), part_dep, part_dep, part_dep)

    def local_step(x_in, ln_scale, ln_shift, w_up, b_up, w_down, b_down, y_grad):
        row_width = x_in.shape[1] * dep_size
        x_float = x_in.astype(jnp.float32)
        row_stats = jnp.stack([jnp.sum(x_float, axis=1), jnp.sum(x_float * x_float, axis=1)], axis=1)
        row_stats = lax.psum(row_stats, "dep")
        mean_row = row_stats[:, 0:1] / row_width
        var_row = row_stats[:, 1:2] / row_width - mean_row * mean_row
        inv_std = lax.rsqrt(var_row + LN_EPS)
        x_hat = (x_float - mean_row) * inv_std
        normed = (x_hat * ln_scale + ln_shift).astype(jnp.bfloat16)
        normed_full = lax.all_gather(normed, "col", axis=0, tiled=True)
        w_up_full = lax.all_gather(w_up, "row", axis=0, tiled=True)
        pre_part = jnp.dot(normed_full, w_up_full, preferred_element_type=jnp.float32)
        pre_act = lax.psum_scatter(pre_part, "dep", scatter_dimension=0, tiled=True) + b_up.astype(jnp.float32)
        hidden = gelu_tanh(pre_act).astype(jnp.bfloat16)
        hidden_full = lax.all_gather(hidden, "dep", axis=0, tiled=True)
        w_down_full = lax.all_gather(w_down, "row", axis=0, tiled=True)
        out_part = jnp.dot(hidden_full, w_down_full, preferred_element_type=jnp.float32)
        out_sum = lax.psum_scatter(out_part, "col", scatter_dimension=0, tiled=True)
        y_out = (x_float + out_sum + b_down.astype(jnp.float32)).astype(jnp.bfloat16)

        g_float = y_grad.astype(jnp.float32)
        grad_full = lax.all_gather(y_grad, "col", axis=0, tiled=True)
        b_down_grad = lax.psum(jnp.sum(g_float, axis=0), ("row", "col"))
        w_down_part = jnp.einsum("tf,td->fd", hidden_full, grad_full, preferred_element_type=jnp.float32)
        w_down_grad = lax.psum_scatter(w_down_part, "row", scatter_dimension=0, tiled=True).astype(jnp.bfloat16)
        hid_part = jnp.einsum("td,fd->tf", grad_full, w_down_full, preferred_element_type=jnp.float32)
        hid_grad = lax.psum_scatter(hid_part, "dep", scatter_dimension=0, tiled=True)
        pre_grad = hid_grad * gelu_slope(pre_act)
        b_up_grad = lax.psum(jnp.sum(pre_grad, axis=0), ("row", "dep"))
        pre_lowp = pre_grad.astype(jnp.bfloat16)
        pre_full = lax.all_gather(pre_lowp, "dep", axis=0, tiled=True)
        w_up_part = jnp.einsum("td,tf->df", normed_full, pre_full, preferred_element_type=jnp.float32)
        w_up_grad = lax.psum_scatter(w_up_part, "row", scatter_dimension=0, tiled=True).astype(jnp.bfloat16)
        norm_part = jnp.einsum("tf,df->td", pre_full, w_up_full, preferred_element_type=jnp.float32)
        norm_grad = lax.psum_scatter(norm_part, "col", scatter_dimension=0, tiled=True)
        value_a9 = norm_grad * ln_scale
        grad_stats = jnp.stack([jnp.sum(value_a9, axis=1), jnp.sum(value_a9 * x_hat, axis=1)], axis=1)
        grad_stats = lax.psum(grad_stats, "dep")
        x_grad = (g_float + inv_std * (value_a9 - grad_stats[:, 0:1] / row_width - x_hat * (grad_stats[:, 1:2] / row_width))).astype(jnp.bfloat16)
        gain_sums = lax.psum(jnp.stack([jnp.sum(norm_grad * x_hat, axis=0), jnp.sum(norm_grad, axis=0)]), ("row", "col"))
        return (y_out, x_grad, w_up_grad, b_up_grad, w_down_grad, b_down_grad, gain_sums[0], gain_sums[1])

    return jax.shard_map(local_step, mesh=mesh, in_specs=in_specs, out_specs=out_specs, check_vma=False)
```

profile of v0, /device:TPU:0, one launch (start us, length us, event | category | flops | bytes accessed | tf_op | source)
XLA Modules:
  0.0 1502.5 jit_solution(14272552573362296465)
XLA Ops:
  7.2 2.6 convert_reduce_fusion
  9.8 3.0 psum.35
  13.5 4.3 fusion.8
  17.8 0.7 all-gather.9.cloned.1.call-update
  18.5 0.7 all-gather.15.cloned.1.call-update
  19.8 66.6 %all-gather.7.cloned.1.call-done = bf16[2048,1280]{1,0:T(8,128)(2,1)} async-done(((bf16[1024,1280]{1,0:T(8,128)(2,1)}), bf16[2048,1280]{1,0:T(8,128)(2,1)}) %all-gather.7.cloned.1.call-update) | async-done | bytes 5242896 | tf_op jit(solution)/shard_map/all_gather | solution.py:40
  86.4 157.9 %all-gather.9.cloned.1.call-done = bf16[1280,5120]{1,0:T(8,128)(2,1)} async-done(((bf16[640,5120]{1,0:T(8,128)(2,1)}), bf16[1280,5120]{1,0:T(8,128)(2,1)}) %all-gather.9.cloned.1.call-update) | async-done | bytes 13107216 | tf_op jit(solution)/shard_map/all_gather | solution.py:41
  244.3 34.7 %fusion.17 = f32[2048,5120]{1,0:T(8,128)} fusion(bf16[2048,1280]{1,0:T(8,128)(2,1)} %all-gather.7.cloned.1.call-done, bf16[1280,5120]{1,0:T(8,128)(2,1)} %all-gather.9.cloned.1.call-done), kind=kOutput, calls=%fused_computation.37 | convolution fusion | flops 26843545600 | bytes 60293120 | tf_op jit(solution)/shard_map/dot_general | solution.py:42
  279.2 32.8 %all-gather.15.cloned.1.call-done = bf16[2048,1280]{1,0:T(8,128)(2,1)} async-done(((bf16[1024,1280]{1,0:T(8,128)(2,1)}), bf16[2048,1280]{1,0:T(8,128)(2,1)}) %all-gather.15.cloned.1.call-update) | async-done | bytes 5242896 | tf_op jit(solution)/shard_map/all_gather | solution.py:52
  312.0 157.7 %all-gather.13.cloned.1.call-done = bf16[5120,1280]{1,0:T(8,128)(2,1)} async-done(((bf16[2560,1280]{1,0:T(8,128)(2,1)}), bf16[5120,1280]{1,0:T(8,128)(2,1)}) %all-gather.13.cloned.1.call-update) | async-done | bytes 13107216 | tf_op jit(solution)/shard_map/all_gather | solution.py:46
  469.7 34.8 %fusion.19 = f32[2048,5120]{1,0:T(8,128)} fusion(bf16[2048,1280]{1,0:T(8,128)(2,1)} %all-gather.15.cloned.1.call-done, bf16[5120,1280]{1,0:T(8,128)(2,1)} %all-gather.13.cloned.1.call-done), kind=kOutput, calls=%fused_computation.39 | convolution fusion | flops 26843545600 | bytes 60293120 | tf_op jit(solution)/shard_map/td,fd->tf/dot_general | solution.py:56
  505.3 10.9 reduce-scatter.21.cloned.1.call-done
  516.2 47.6 %reduce-scatter.23.cloned.1.call-done = f32[1024,5120]{1,0:T(8,128)} async-done(((f32[2048,5120]{1,0:T(8,128)}), f32[1024,5120]{1,0:T(8,128)}) %reduce-scatter.23.cloned.1.call-update) | async-done | bytes 20971536
  563.8 28.3 %fusion.16 = (f32[5120]{0:T(1024)}, bf16[1024,5120]{1,0:T(8,128)(2,1)}, bf16[1024,5120]{1,0:T(8,128)(2,1)}) fusion(f32[1024,5120]{1,0:T(8,128)} %reduce-scatter.23.cloned.1.call-done, f32[1024,5120]{1,0:T(8,128)} %reduce-scatter.21.cloned.1.call-done, f32[5120]{0:T(1024)S(1)} %convert_element_type.35), kind=kLoop, calls=%fused_computation.36 | loop fusion | flops 115338240 | bytes 62955520 | tf_op jit(solution)/shard_map/reduce_sum | solution.py:59
  592.1 0.7 all-gather.11.cloned.1.call-update
  593.1 33.7 %all-gather.17.cloned.1.call-done = bf16[2048,5120]{1,0:T(8,128)(2,1)} async-done(((bf16[1024,5120]{1,0:T(8,128)(2,1)}), bf16[2048,5120]{1,0:T(8,128)(2,1)}) %all-gather.17.cloned.1.call-update) | async-done | bytes 20971536 | tf_op jit(solution)/shard_map/all_gather | solution.py:61
  626.7 35.7 %fusion.20 = f32[2048,1280]{1,0:T(8,128)} fusion(bf16[2048,5120]{1,0:T(8,128)(2,1)} %all-gather.17.cloned.1.call-done, bf16[1280,5120]{1,0:T(8,128)(2,1)} %all-gather.9.cloned.1.call-done), kind=kOutput, calls=%fused_computation.40 | convolution fusion | flops 26843545600 | bytes 44564480 | tf_op jit(solution)/shard_map/tf,df->td/dot_general | solution.py:64
  662.9 35.4 %fusion.18 = f32[2048,1280]{1,0:T(8,128)} fusion(bf16[2048,5120]{1,0:T(8,128)(2,1)} %all-gather.11.cloned.1.call-done, bf16[5120,1280]{1,0:T(8,128)(2,1)} %all-gather.13.cloned.1.call-done), kind=kOutput, calls=%fused_computation.38 | convolution fusion | flops 26843545600 | bytes 44564480 | tf_op jit(solution)/shard_map/dot_general | solution.py:47
  698.6 34.4 %fusion.21 = f32[1280,5120]{1,0:T(8,128)} fusion(bf16[2048,1280]{1,0:T(8,128)(2,1)} %all-gather.7.cloned.1.call-done, bf16[2048,5120]{1,0:T(8,128)(2,1)} %all-gather.17.cloned.1.call-done), kind=kOutput, calls=%fused_computation.41 | convolution fusion | flops 26843545600 | bytes 52428800 | tf_op jit(solution)/shard_map/td,tf->df/dot_general | solution.py:62
  733.1 34.7 %fusion.22 = f32[5120,1280]{1,0:T(8,128)} fusion(bf16[2048,5120]{1,0:T(8,128)(2,1)} %all-gather.11.cloned.1.call-done, bf16[2048,1280]{1,0:T(8,128)(2,1)} %all-gather.15.cloned.1.call-done), kind=kOutput, calls=%fused_computation.42 | convolution fusion | flops 26843545600 | bytes 52428800 | tf_op jit(solution)/shard_map/tf,td->fd/dot_general | solution.py:54
  768.6 13.6 psum.37
  782.2 3.2 reduce-scatter.15.cloned.1.call-done
  785.4 4.3 fusion.12
  789.8 2.5 psum.36
  792.3 114.3 %reduce-scatter.13.cloned.1.call-done = f32[1024,1280]{1,0:T(8,128)} async-done(((f32[2048,1280]{1,0:T(8,128)}), f32[1024,1280]{1,0:T(8,128)}) %reduce-scatter.13.cloned.1.call-update) | async-done | bytes 5242896 | tf_op jit(solution)/shard_map/reduce_scatter | solution.py:48
  906.6 7.8 convert_reduce_fusion.1
  914.4 15.8 %all-reduce.2 = (f32[1280]{0:T(1024)}, f32[2,1280]{1,0:T(2,128)S(1)}) all-reduce(f32[1280]{0:T(1024)S(1)} %get-tuple-element.21, f32[2,1280]{1,0:T(2,128)S(1)} %pad_maximum_fusion), channel_id=1, replica_groups=mesh['part'=1,'row'=2,'col'=2,'dep'=2] {'row','col'}, use_global_device_ids=true, to_apply=%region_15.0 | all-reduce | flops 3840 | bytes 30720 | tf_op jit(solution)/shard_map/psum | solution.py:53
  930.2 0.6 slice_reduce_fusion
  930.8 266.5 %reduce-scatter.17.cloned.1.call-done = f32[640,5120]{1,0:T(8,128)} async-done(((f32[1280,5120]{1,0:T(8,128)}), f32[640,5120]{1,0:T(8,128)}) %reduce-scatter.17.cloned.1.call-update) | async-done | bytes 13107216 | tf_op jit(solution)/shard_map/reduce_scatter | solution.py:63
  1197.3 8.5 convert_element_type.42
  1205.8 281.3 %reduce-scatter.19.cloned.1.call-done = f32[2560,1280]{1,0:T(8,128)} async-done(((f32[5120,1280]{1,0:T(8,128)}), f32[2560,1280]{1,0:T(8,128)}) %reduce-scatter.19.cloned.1.call-update) | async-done | bytes 13107216 | tf_op jit(solution)/shard_map/reduce_scatter | solution.py:55
  1487.1 8.1 convert_element_type.43
  (49 shorter events, 4.2 us)
Async XLA Ops:
  7.2 79.2 %all-gather.7.cloned.1.call-start = ((), (), s32[]{:S(2)}) async-start(), calls=%async_computation.6 | async-start | bytes 7864320 | tf_op jit(solution)/shard_map/all_gather | solution.py:40
  12.8 0.6 copy-start.3
  12.9 0.6 copy-start.5
  17.7 226.5 %all-gather.9.cloned.1.call-start = ((), (), s32[]{:S(2)}) async-start(), calls=%async_computation.7 | async-start | bytes 19660800 | tf_op jit(solution)/shard_map/all_gather | solution.py:41
  18.5 293.5 %all-gather.15.cloned.1.call-start = ((), (), s32[]{:S(2)}) async-start(), calls=%async_computation.11 | async-start | bytes 7864320 | tf_op jit(solution)/shard_map/all_gather | solution.py:52
  19.2 450.5 %all-gather.13.cloned.1.call-start = ((), (), s32[]{:S(2)}) async-start(), calls=%async_computation.9 | async-start | bytes 19660800 | tf_op jit(solution)/shard_map/all_gather | solution.py:46
  19.8 496.4 %reduce-scatter.21.cloned.1.call-start = ((), (), s32[]{:S(2)}) async-start(), calls=%async_computation.16 | async-start | bytes 62914560
  279.0 284.8 %reduce-scatter.23.cloned.1.call-start = ((), (), s32[]{:S(2)}) async-start(), calls=%async_computation.17 | async-start | bytes 62914560
  504.6 0.7 copy-start.7
  504.6 122.2 %all-gather.17.cloned.1.call-start = ((), (), s32[]{:S(2)}) async-start(), calls=%async_computation.12 | async-start | bytes 31457280 | tf_op jit(solution)/shard_map/all_gather | solution.py:61
  592.1 70.8 %all-gather.11.cloned.1.call-start = ((), (), s32[]{:S(2)}) async-start(), calls=%async_computation.8 | async-start | bytes 31457280 | tf_op jit(solution)/shard_map/all_gather | solution.py:45
  592.8 192.6 %reduce-scatter.15.cloned.1.call-start = ((), (), s32[]{:S(2)}) async-start(), calls=%async_computation.13 | async-start | bytes 15728640 | tf_op jit(solution)/shard_map/reduce_scatter | solution.py:65
  662.4 244.2 %reduce-scatter.13.cloned.1.call-start = ((), (), s32[]{:S(2)}) async-start(), calls=%async_computation.10 | async-start | bytes 15728640 | tf_op jit(solution)/shard_map/reduce_scatter | solution.py:48
  698.3 499.0 %reduce-scatter.17.cloned.1.call-start = ((), (), s32[]{:S(2)}) async-start(), calls=%async_computation.14 | async-start | bytes 39321600 | tf_op jit(solution)/shard_map/reduce_scatter | solution.py:63
  733.0 754.0 %reduce-scatter.19.cloned.1.call-start = ((), (), s32[]{:S(2)}) async-start(), calls=%async_computation.15 | async-start | bytes 39321600 | tf_op jit(solution)/shard_map/reduce_scatter | solution.py:55
  767.8 0.7 copy-start.8
  767.8 0.7 copy-start.1
  767.8 17.6 %copy-start = (bf16[1024,1280]{1,0:T(8,128)(2,1)S(1)}, bf16[1024,1280]{1,0:T(8,128)(2,1)}, u32[]{:S(2)}) copy-start(bf16[1024,1280]{1,0:T(8,128)(2,1)} %param.8) | copy-start | bytes 7864324
  767.8 17.6 %copy-start.2 = (f32[1280]{0:T(1024)S(1)}, f32[1280]{0:T(1024)}, u32[]{:S(2)}) copy-start(f32[1280]{0:T(1024)} %param.9) | copy-start | bytes 15364
  767.9 17.6 %copy-start.4 = (f32[1024,1]{0,1:T(1,128)S(1)}, f32[1024,1]{0,1:T(1,128)}, u32[]{:S(2)}) copy-start(f32[1024,1]{0,1:T(1,128)} %copy-done.3) | copy-start | bytes 12292
  767.9 17.6 %copy-start.6 = (f32[1024,1]{0,1:T(1,128)S(1)}, f32[1024,1]{0,1:T(1,128)}, u32[]{:S(2)}) copy-start(f32[1024,1]{0,1:T(1,128)} %copy-done.5) | copy-start | bytes 12292
Sparse Core Ops, SparseCore 0:
  17.9 68.4 all-gather.6
  87.9 156.3 all-gather.8
  245.8 66.1 all-gather.14
  313.4 156.3 all-gather.12
  471.9 44.3 reduce-scatter.20
  518.3 45.4 reduce-scatter.22
  592.2 34.5 all-gather.16
  628.3 34.5 all-gather.10
  665.1 120.2 reduce-scatter.14
  787.5 119.0 reduce-scatter.12
  908.9 288.3 reduce-scatter.16
  1199.4 287.5 reduce-scatter.18
where the time goes:
time: 1510 us; the launch traced here: 1500 us
  waiting for transfers between devices  1180 us (78%)
  matrix products  210 us (14%)
  other arithmetic  63.9 us (4%)
  blocking collectives  35 us (2%)
    reduce_scatter x1, waiting for transfers between devices, local_step(): lax.psum_scatter(w_down_part, 'row', scatter_dimension=0, tiled=True)  281 us
    reduce_scatter x1, waiting for transfers between devices, local_step(): lax.psum_scatter(w_up_part, 'row', scatter_dimension=0, tiled=True)  266 us
    all_gather x1, waiting for transfers between devices, local_step(): w_up_full = lax.all_gather(w_up, 'row', axis=0, tiled=True)  158 us
    all_gather x1, waiting for transfers between devices, local_step(): w_down_full = lax.all_gather(w_down, 'row', axis=0, tiled=True)  158 us
    reduce_scatter x1, waiting for transfers between devices, local_step(): out_sum = lax.psum_scatter(out_part, 'col', scatter_dimension=0, tiled=True)  114 us
    all_gather x1, waiting for transfers between devices, local_step(): normed_full = lax.all_gather(normed, 'col', axis=0, tiled=True)  66.6 us
    unnamed x14, waiting for transfers between devices  61.2 us
    dot_general x1, matrix products, local_step(): jnp.einsum('tf,df->td', pre_full, w_up_full, preferred_element_type=jnp.f...  35.7 us
  transfers between devices with their start and end apart: 12, of which 12 were waited for; matrix products, arithmetic and copies ran while one was open for 15% of the time, Pallas kernels for 0%

commit v1 on v0

v1 whole, which is shorter than its diff:
```python
import functools
import jax
import jax.numpy as jnp
from jax import lax
from jax.experimental import pallas as pl
from jax.experimental.pallas import tpu as pltpu
from jax.sharding import PartitionSpec as P

LN_EPS = 1e-5
GELU_K = 0.7978845608028654
GELU_C = 0.044715
SWAP = [(0, 1), (1, 0)]
CROSS = [(0, 3), (1, 2), (2, 1), (3, 0)]
f32 = jnp.float32
bf16 = jnp.bfloat16
VMEM_LIMIT = 60 * 1024 * 1024
CH_ACT = 256
CH_OUT = 1280
CH_GRAD = 256


def gelu_both(c):
    sq = c * c
    t = jnp.tanh(c * (GELU_K + (GELU_K * GELU_C) * sq))
    half = 0.5 * c
    h = half + half * t
    s = (0.5 + 0.5 * t) + half * (1.0 - t * t) * (GELU_K + (3.0 * GELU_K * GELU_C) * sq)
    return h, s


def mm(a, b):
    return lax.dot_general(a, b, (((1,), (0,)), ((), ())), preferred_element_type=f32)


def mmt(a, b):
    return lax.dot_general(a, b, (((1,), (1,)), ((), ())), preferred_element_type=f32)


def side(u, v):
    return jnp.concatenate([u[...], v[...]], axis=1)


def run_copies(copies, sems):
    descs = [pltpu.make_async_copy(s, d, sems.at[i]) for i, (s, d) in enumerate(copies)]
    for c in descs:
        c.start()
    for c in descs:
        c.wait()


def tile_map(b, nb, i, *_):
    return (jnp.clip(i - b * nb, 0, nb - 1), 0)


HBM = pl.BlockSpec(memory_space=pl.ANY)


def tiled_call(body, idx, blocks_in, weights, consts, blocks_out, sums_out, scratch, bm, flops):
    nblk = len(blocks_in)
    n = blocks_in[0][0].shape[0]
    nb = n // bm
    ins, in_specs, outs, out_specs = [], [], [], []
    for b, arrs in enumerate(blocks_in):
        for a in arrs:
            ins.append(a)
            in_specs.append(pl.BlockSpec((bm, a.shape[1]), functools.partial(tile_map, b, nb)))
    for w in weights:
        ins.append(w)
        in_specs.append(HBM)
    for c in consts:
        ins.append(c)
        in_specs.append(pl.BlockSpec(c.shape, lambda i, *_: (0, 0)))
    for b in range(nblk):
        for shp in blocks_out:
            outs.append(jax.ShapeDtypeStruct((n, shp[0]), shp[1]))
            out_specs.append(pl.BlockSpec((bm, shp[0]), functools.partial(tile_map, b, nb)))
    for shp in sums_out:
        outs.append(jax.ShapeDtypeStruct(shp, f32))
        out_specs.append(pl.BlockSpec(shp, lambda i, *_: (0, 0)))
    na, no = len(blocks_in[0]), len(blocks_out)

    def kernel(idx_ref, *refs):
        i = pl.program_id(0)
        at = 0
        tin = [refs[b * na:(b + 1) * na] for b in range(nblk)]
        at = na * nblk
        wr = refs[at:at + len(weights)]
        at += len(weights)
        cr = refs[at:at + len(consts)]
        at += len(consts)
        tout = [refs[at + b * no:at + (b + 1) * no] for b in range(nblk)]
        at += no * nblk
        sr = refs[at:at + len(sums_out)]
        at += len(sums_out)
        scr, sems = refs[at:-1], refs[-1]
        load, step = body

        @pl.when(i == 0)
        def _():
            run_copies(load(idx_ref[0], idx_ref[1], wr, scr), sems)
            for s in sr:
                s[...] = jnp.zeros_like(s)

        for b in range(nblk):
            @pl.when(i // nb == b)
            def _(b=b):
                step(tin[b], cr, tout[b], sr, scr)

    call = pl.pallas_call(
        kernel,
        out_shape=outs,
        grid_spec=pltpu.PrefetchScalarGridSpec(
            num_scalar_prefetch=1, grid=(nblk * nb,), in_specs=in_specs, out_specs=out_specs,
            scratch_shapes=list(scratch) + [pltpu.SemaphoreType.DMA((32,))]),
        compiler_params=pltpu.CompilerParams(dimension_semantics=("arbitrary",), vmem_limit_bytes=VMEM_LIMIT),
        cost_estimate=pl.CostEstimate(flops=flops, bytes_accessed=1 << 24, transcendentals=0),
    )
    return call(idx, *ins)


def col_at(ref, start, size):
    return ref.at[:, pl.ds(pl.multiple_of(start, 128), size)]


def row_at(ref, start, size):
    return ref.at[pl.ds(pl.multiple_of(start, 8), size), :]


def act_call(mode, idx, blocks, groups, w_up, w_down, biases, bm, with_sums):
    fe = w_up.shape[1] // 4
    q = w_up.shape[0]
    dm = 4 * q
    ng = len(groups)
    has_c, has_d = "c" in mode, "d" in mode
    weights = [w_up, w_down]
    for _, p1, p2 in groups:
        weights += (list(p1) if has_c else []) + (list(p2) if has_d else [])

    def load(r, k, wr, scr):
        up, down = wr[0], wr[1]
        rest = list(wr[2:])
        bufs = list(scr)
        copies = []
        for own, p1, p2 in groups:
            if has_c:
                buf = bufs.pop(0)
                rr = r if own else 1 - r
                dep, row, cross = rest.pop(0), rest.pop(0), rest.pop(0)
                copies += [(col_at(up, (rr * 2 + k) * fe, fe), row_at(buf, r * q, q)),
                           (row, row_at(buf, (1 - r) * q, q)),
                           (dep, row_at(buf, 2 * q + r * q, q)),
                           (cross, row_at(buf, 2 * q + (1 - r) * q, q))]
            if has_d:
                buf = bufs.pop(0)
                if own:
                    dep = rest.pop(0)
                    copies += [(row_at(down, k * fe, fe), buf.at[:, 0:2 * q]), (dep, buf.at[:, 2 * q:4 * q])]
                else:
                    for j in range(4):
                        copies.append((rest.pop(0), buf.at[:, j * q:(j + 1) * q]))
        return copies

    def step(tin, cr, tout, sr, scr):
        tin, bufs = list(tin), list(scr)
        u, v = (tin.pop(0), tin.pop(0)) if has_c else (None, None)
        gu, gv = (tin.pop(0), tin.pop(0)) if has_d else (None, None)
        tout = list(tout)
        for g in range(ng):
            w1 = bufs.pop(0) if has_c else None
            w2 = bufs.pop(0) if has_d else None
            s_in = tin.pop(0) if not has_c else None
            h_out = tout.pop(0) if has_c else None
            x_out = tout.pop(0)
            for n0 in range(0, fe, CH_ACT):
                sl = slice(n0, n0 + CH_ACT)
                if has_c:
                    c = mm(side(u, v), w1[:, sl]) + cr[g][:, sl]
                    h, s = gelu_both(c)
                    h_out[:, sl] = h.astype(bf16)
                else:
                    s = s_in[:, sl]
                if has_d:
                    p = mmt(side(gu, gv), w2[sl, :]) * s
                    x_out[:, sl] = p.astype(bf16)
                    if with_sums:
                        sr[g][:, sl] += jnp.sum(p, axis=0, keepdims=True)
                else:
                    x_out[:, sl] = s

    scratch = []
    for _ in range(ng):
        scratch += [pltpu.VMEM((dm, fe), bf16)] if has_c else []
        scratch += [pltpu.VMEM((fe, dm), bf16)] if has_d else []
    outs = []
    for _ in range(ng):
        outs += [(fe, bf16)] if has_c else []
        outs += [(fe, bf16)] if has_d else [(fe, f32)]
    n = blocks[0][0].shape[0]
    flops = 2 * n * len(blocks) * dm * fe * ng * (int(has_c) + int(has_d))
    res = tiled_call((load, step), idx, blocks, weights, [b.reshape(1, fe) for b in biases] if has_c else [],
                     outs, [(1, fe)] * ng if with_sums else [], scratch, bm, flops)
    no = len(outs)
    per = [res[b * no:(b + 1) * no] for b in range(len(blocks))]
    return per, res[no * len(blocks):]


def out_call(idx, blocks, weights, load_fn, transposed, q, fe, bm):
    shape = (2 * q, 2 * fe) if transposed else (2 * fe, 2 * q)

    def load(r, k, wr, scr):
        return load_fn(r, k, wr, scr[0])

    def step(tin, cr, tout, sr, scr):
        o, n = tin
        w = scr[0]
        for n0 in range(0, 2 * q, CH_OUT):
            n1 = n0 + CH_OUT
            y = mmt(side(o, n), w[n0:n1, :]) if transposed else mm(side(o, n), w[:, n0:n1])
            if n0 < q:
                tout[0][:, n0:min(n1, q)] = y[:, :min(n1, q) - n0]
            if n1 > q:
                m = max(q - n0, 0)
                tout[1][:, n0 + m - q:n1 - q] = y[:, m:]

    flops = 2 * blocks[0][0].shape[0] * len(blocks) * 2 * q * 2 * fe
    res = tiled_call((load, step), idx, blocks, weights, [], [(q, f32), (q, f32)], [], [pltpu.VMEM(shape, bf16)], bm, flops)
    return [res[2 * b:2 * b + 2] for b in range(len(blocks))]


def grad_call(idx, lhs, rhs, acc, out_dtype, halves):
    nblk = len(rhs)
    n = rhs[0][0].shape[0]
    fe = rhs[0][0].shape[1]
    m = fe
    ng = len(rhs[0])
    nt = fe // CH_GRAD
    ins, in_specs = [], []
    for parts in lhs:
        for p in parts:
            ins.append(p)
            if halves:
                in_specs.append(pl.BlockSpec((n, m // 2), lambda j, s: (0, s[0]), pipeline_mode=pl.Buffered(1)))
            else:
                in_specs.append(pl.BlockSpec((n, m), lambda j, s: (0, 0), pipeline_mode=pl.Buffered(1)))
    for parts in rhs:
        for p in parts:
            ins.append(p)
            in_specs.append(pl.BlockSpec((n, CH_GRAD), lambda j, s: (0, j)))
    for p in acc:
        ins.append(p)
        in_specs.append(pl.BlockSpec((m, CH_GRAD), lambda j, s: (0, j)))
    nl = len(lhs[0])

    def kernel(idx_ref, *refs):
        lr = refs[:nl * nblk]
        rr = refs[nl * nblk:nl * nblk + ng * nblk]
        ar = refs[nl * nblk + ng * nblk:nl * nblk + ng * nblk + len(acc)]
        outs, scr = refs[-1 - ng:-1], refs[-1]

        @pl.when(pl.program_id(0) == 0)
        def _():
            for b in range(nblk):
                for p in range(nl):
                    w = m // nl
                    scr[p * w:(p + 1) * w, b * n:(b + 1) * n] = lr[b * nl + p][...].T

        for g in range(ng):
            y = mm(scr[...], jnp.concatenate([rr[b * ng + g][...] for b in range(nblk)], axis=0))
            if acc:
                y = y + ar[g][...]
            outs[g][...] = y.astype(out_dtype)

    res = pl.pallas_call(
        kernel,
        out_shape=[jax.ShapeDtypeStruct((m, fe), out_dtype)] * ng,
        grid_spec=pltpu.PrefetchScalarGridSpec(
            num_scalar_prefetch=1, grid=(nt,), in_specs=in_specs,
            out_specs=[pl.BlockSpec((m, CH_GRAD), lambda j, s: (0, j))] * ng,
            scratch_shapes=[pltpu.VMEM((m, nblk * n), bf16)]),
        compiler_params=pltpu.CompilerParams(dimension_semantics=("arbitrary",), vmem_limit_bytes=VMEM_LIMIT),
        cost_estimate=pl.CostEstimate(flops=2 * n * nblk * m * fe * ng, bytes_accessed=1 << 24, transcendentals=0),
    )(idx, *ins)
    return res


def solution(mesh):
    dep_size = mesh.shape["dep"]
    tok_spec = P(("part", "row", "col"), "dep")
    vec_dep = P("dep")
    part_dep = P(("part", "dep"))
    in_specs = (tok_spec, vec_dep, vec_dep, P(("dep", "row"), "col"), P("col"), P(("col", "row"), "dep"), vec_dep, tok_spec)
    out_specs = (tok_spec, tok_spec, P(("part", "dep", "row"), "col"), P(("part", "col")), P(("part", "col", "row"), "dep"), part_dep, part_dep, part_dep)

    def px(v):
        return lax.ppermute(v, "col", SWAP)

    def py(v):
        return lax.ppermute(v, "row", SWAP)

    def pd(v):
        return lax.ppermute(v, "dep", SWAP)

    def pyd(v):
        return lax.ppermute(v, ("row", "dep"), CROSS)

    def local_step(x_in, ln_scale, ln_shift, w_up, b_up, w_down, b_down, y_grad):
        r = lax.axis_index("row")
        k = lax.axis_index("dep")
        idx = jnp.stack([r, k]).astype(jnp.int32)
        _, dh_ = x_in.shape
        q = dh_ // 2
        fe = w_up.shape[1] // 4
        row_width = dh_ * dep_size

        def cols(rr, kk):
            return lax.dynamic_slice_in_dim(w_up, (rr * 2 + kk) * fe, fe, axis=1)

        def rows(kk):
            return lax.dynamic_slice_in_dim(w_down, kk * fe, fe, axis=0)

        def bias(rr):
            return lax.dynamic_slice_in_dim(b_up, (rr * 2 + k) * fe, fe, axis=0).astype(f32)

        gx = px(y_grad)
        own_o, own_n, snd_o, snd_n = cols(r, k), cols(1 - r, k), cols(r, 1 - k), cols(1 - r, 1 - k)
        w1o = (pd(snd_o), py(own_n), pyd(snd_n))
        w1n = (pd(snd_n), py(own_o), pyd(snd_o))
        rk, rk2 = rows(k), rows(1 - k)
        w2o = (pd(rk2),)
        own0, oth0 = py(rk[:, :q]), pyd(rk2[:, :q])
        own1, oth1 = py(rk[:, q:]), pyd(rk2[:, q:])
        w2n = (own0, own1, oth0, oth1)
        bo, bn = bias(r), bias(1 - r)

        x_float = x_in.astype(f32)
        row_stats = jnp.stack([jnp.sum(x_float, axis=1), jnp.sum(x_float * x_float, axis=1)], axis=1)
        row_stats = lax.psum(row_stats, "dep")
        mean_row = row_stats[:, 0:1] / row_width
        var_row = row_stats[:, 1:2] / row_width - mean_row * mean_row
        inv_std = lax.rsqrt(var_row + LN_EPS)
        x_hat = (x_float - mean_row) * inv_std
        a0 = (x_hat * ln_scale + ln_shift).astype(bf16)
        ax, ay = px(a0), py(a0)
        gy = py(y_grad)
        ad, gd = py(ax), px(gy)

        def half(u):
            return (u, pd(u))

        A = [half(a0), half(ax), half(ay), half(ad)]
        G = [half(y_grad), half(gx), half(gy), half(gd)]
        go, gn = (True, w1o, w2o), (False, w1n, w2n)

        def act(mode, blocks, groups, biases, bm, sums):
            return act_call(mode, idx, blocks, groups, w_up, w_down, biases, bm, sums)

        (o0, ox), (sum_o,) = act("cd", [A[0] + G[0], A[1] + G[1]], [go], [bo], 512, True)
        (n0, nx), _ = act("c", [A[0], A[1]], [gn], [bn], 512, False)
        dw2 = grad_call(idx, [[o0[0]], [ox[0]]], [G[0], G[1]], [], f32, False)
        dw1o = grad_call(idx, [A[0], A[1]], [[o0[1]], [ox[1]]], [], f32, True)

        def reduce_out(parts):
            (own_a, oth_a), (own_x, oth_x) = parts
            send = own_x + pd(oth_x)
            return own_a + pd(oth_a) + px(send)

        def y_load(j):
            def load(rr, kk, wr, buf):
                down, dep, a, b = wr
                return [(down.at[pl.ds(pl.multiple_of(kk * fe, 8), fe), j * q:(j + 1) * q], buf.at[0:fe, 0:q]),
                        (dep.at[:, j * q:(j + 1) * q], buf.at[0:fe, q:2 * q]),
                        (a, buf.at[fe:2 * fe, 0:q]), (b, buf.at[fe:2 * fe, q:2 * q])]

            return load

        hs = [(o0[0], n0[0]), (ox[0], nx[0])]
        y_parts = []
        for j, (own, oth) in enumerate(((own0, oth0), (own1, oth1))):
            res = out_call(idx, hs, [w_down, w2o[0], own, oth], y_load(j), False, q, fe, 512)
            y_parts.append(reduce_out(res))
        y_out = (x_float + jnp.concatenate(y_parts, axis=1) + b_down.astype(f32)).astype(bf16)

        (m0, mx), (sum_n,) = act("d", [tuple(G[0]) + (n0[1],), tuple(G[1]) + (nx[1],)], [gn], [], 512, True)

        def da_load_own(rr, kk, wr, buf):
            up, do, dn = wr
            return [(col_at(up, (rr * 2 + kk) * fe, fe), buf.at[0:q, 0:fe]), (col_at(up, ((1 - rr) * 2 + kk) * fe, fe), buf.at[0:q, fe:2 * fe]),
                    (do, buf.at[q:2 * q, 0:fe]), (dn, buf.at[q:2 * q, fe:2 * fe])]

        def da_load_oth(rr, kk, wr, buf):
            a, b, do, dn = wr
            return [(a, buf.at[0:q, 0:fe]), (b, buf.at[0:q, fe:2 * fe]), (do, buf.at[q:2 * q, 0:fe]), (dn, buf.at[q:2 * q, fe:2 * fe])]

        ds = [(o0[1], m0[0]), (ox[1], mx[0])]
        res = out_call(idx, ds, [w_up, w1o[0], w1n[0]], da_load_own, True, q, fe, 512)
        na = reduce_out(res)
        res = out_call(idx, ds, [w1o[1], w1n[1], w1o[2], w1n[2]], da_load_oth, True, q, fe, 512)
        nb = reduce_out(res)
        norm_grad = jnp.where(r == 0, jnp.concatenate([na, nb], axis=1), jnp.concatenate([nb, na], axis=1))
        value = norm_grad * ln_scale
        grad_stats = jnp.stack([jnp.sum(value, axis=1), jnp.sum(value * x_hat, axis=1)], axis=1)
        grad_stats = lax.psum(grad_stats, "dep")
        dx = inv_std * (value - grad_stats[:, 0:1] / row_width - x_hat * (grad_stats[:, 1:2] / row_width))
        x_grad = (y_grad.astype(f32) + dx).astype(bf16)
        gains = jnp.stack([jnp.sum(norm_grad * x_hat, axis=0), jnp.sum(norm_grad, axis=0)])

        dw1n = grad_call(idx, [A[0], A[1]], [[m0[0]], [mx[0]]], [], f32, True)
        (py_,), _ = act("cd", [A[2] + G[2]], [go, gn], [bo, bn], 256, False)
        (pz,), _ = act("cd", [A[3] + G[3]], [go, gn], [bo, bn], 256, False)
        dw2 = grad_call(idx, [[py_[0]], [pz[0]]], [G[2], G[3]], dw2, bf16, False)
        dw1o, dw1n = grad_call(idx, [A[2], A[3]], [[py_[1], py_[3]], [pz[1], pz[3]]], [dw1o[0], dw1n[0]], bf16, True)

        ro, rn = pd(dw1o[q:]), pd(dw1n[q:])
        w_up_grad = jnp.zeros(w_up.shape, bf16)
        for v, rr, kk in ((dw1o[:q], r, k), (dw1n[:q], 1 - r, k), (ro, r, 1 - k), (rn, 1 - r, 1 - k)):
            w_up_grad = lax.dynamic_update_slice_in_dim(w_up_grad, v, (rr * 2 + kk) * fe, axis=1)
        mine, other = dw2[0], pd(dw2[1])
        w_down_grad = jnp.zeros(w_down.shape, bf16)
        w_down_grad = lax.dynamic_update_slice_in_dim(w_down_grad, mine, k * fe, axis=0)
        w_down_grad = lax.dynamic_update_slice_in_dim(w_down_grad, other, (1 - k) * fe, axis=0)

        def both(v):
            v = v + px(v)
            return v + py(v)

        b_down_grad = both(jnp.sum(y_grad.astype(f32), axis=0))
        gain_sums = both(gains)
        full = jnp.concatenate([sum_o, sum_n]) + py(jnp.concatenate([sum_n, sum_o]))
        oth = pd(full)
        b_up_grad = jnp.zeros(b_up.shape, f32)
        for v, rr, kk in ((full[0], r, k), (full[1], 1 - r, k), (oth[0], r, 1 - k), (oth[1], 1 - r, 1 - k)):
            b_up_grad = lax.dynamic_update_slice_in_dim(b_up_grad, v, (rr * 2 + kk) * fe, axis=0)
        return (y_out, x_grad, w_up_grad, b_up_grad, w_down_grad, b_down_grad, gain_sums[0], gain_sums[1])

    return jax.shard_map(local_step, mesh=mesh, in_specs=in_specs, out_specs=out_specs, check_vma=False)
```

time: 1510 us -> 938 us (0.62)
  waiting for transfers between devices: 1180 us -> 442 us
  Pallas kernels: 0 us -> 376 us
  matrix products: 210 us -> 0 us
  local copies, waits for them, and re-layouts: 2.55 us -> 39.8 us
  blocking collectives: 35 us -> 5 us
  starting transfers between devices: 1.12 us -> 28 us
  other arithmetic: 63.9 us -> 42.2 us
    reduce_scatter x4 -> x0, waiting for transfers between devices: 665 us -> none  [the longest x1 281 us: local_step(): lax.psum_scatter(w_down_part, 'row', scatter_dimension=0, tiled=True)]
    all_gather x6 -> x0, waiting for transfers between devices: 449 us -> none  [the longest x1 158 us: local_step(): w_up_full = lax.all_gather(w_up, 'row', axis=0, tiled=True)]
    ppermute x0 -> x46, waiting for transfers between devices: none -> 442 us  [the longest x10 181 us: py(): return lax.ppermute(v, 'row', SWAP)]
    pallas_call x0 -> x14, Pallas kernels: none -> 376 us  [the longest x9 280 us: tiled_call(): return call(idx, *ins)]
    dot_general x6 -> x0, matrix products: 210 us -> none  [the longest x1 35.7 us: local_step(): jnp.einsum('tf,df->td', pre_full, w_up_full, preferred_element_type=jnp.f...]
    unnamed x14 -> x0, waiting for transfers between devices: 61.2 us -> none
    psum x2 -> x0, blocking collectives: 29.4 us -> none  [the longest x1 15.8 us: local_step(): b_down_grad = lax.psum(jnp.sum(g_float, axis=0), ('row', 'col'))]
    ppermute x0 -> x46, starting transfers between devices: none -> 28 us  [the longest x9 9.69 us: px(): return lax.ppermute(v, 'col', SWAP)]
  transfers between devices with their start and end apart: 12 -> 46, of which waited for: 12 -> 14; matrix products, arithmetic and copies ran while one was open for 15% -> 7% of each run, Pallas kernels for 0% -> 40%
where the time goes in v1:
time: 938 us; the launch traced here: 934 us
  waiting for transfers between devices  442 us (47%)
  Pallas kernels  376 us (40%)
  other arithmetic  42.2 us (4%)
  local copies, waits for them, and re-layouts  39.8 us (4%)
  starting transfers between devices  28 us (3%)
    pallas_call x9, Pallas kernels, tiled_call(): return call(idx, *ins)  280 us
    ppermute x10, waiting for transfers between devices, py(): return lax.ppermute(v, 'row', SWAP)  181 us
    ppermute x9, waiting for transfers between devices, px(): return lax.ppermute(v, 'col', SWAP)  163 us
    ppermute x4, waiting for transfers between devices, pyd(): return lax.ppermute(v, ('row', 'dep'), CROSS)  97.2 us
    pallas_call x5, Pallas kernels, grad_call(): pl.pallas_call(kernel, out_shape=[jax.ShapeDtypeStruct((m, fe), out_dtype...  95.7 us
  transfers between devices with their start and end apart: 46, of which 14 were waited for; matrix products, arithmetic and copies ran while one was open for 7% of the time, Pallas kernels for 40%

profile of v1, /device:TPU:0, one launch (start us, length us, event | category | flops | bytes accessed | tf_op | source)
XLA Modules:
  0.0 934.1 jit_solution(2405720272703129474)
XLA Ops:
  0.7 6.0 constant_dynamic-slice_fusion.2
  18.6 28.0 %collective-permute-done.12.refs_8_.refs_7_.refs_12_ = bf16[640,1280]{1,0:T(8,128)(2,1)} collective-permute-done((bf16[640,1280]{1,0:T(8,128)(2,1)}, bf16[640,1280]{1,0:T(8,128)(2,1)}, u32[]{:S(2)}, u32[]{:S(2)}) %collective-permute-start.12) | collective-permute-done | bytes 1638432 | tf_op jit(solution)/shard_map/ppermute | solution.py:304
  51.1 30.6 %collective-permute-done.8.refs_12_.refs_6_.refs_8_ = bf16[640,1280]{1,0:T(8,128)(2,1)} collective-permute-done((bf16[640,1280]{1,0:T(8,128)(2,1)}, bf16[640,1280]{1,0:T(8,128)(2,1)}, u32[]{:S(2)}, u32[]{:S(2)}) %collective-permute-start.8) | collective-permute-done | bytes 1638432 | tf_op jit(solution)/shard_map/ppermute | solution.py:304
  82.2 34.8 %collective-permute-done.7.refs_11_.refs_4_.refs_7_ = bf16[640,1280]{1,0:T(8,128)(2,1)} collective-permute-done((bf16[640,1280]{1,0:T(8,128)(2,1)}, bf16[640,1280]{1,0:T(8,128)(2,1)}, u32[]{:S(2)}, u32[]{:S(2)}) %collective-permute-start.7) | collective-permute-done | bytes 1638432 | tf_op jit(solution)/shard_map/ppermute | solution.py:298
  117.5 13.9 %collective-permute-done.4.refs_6_.refs_3_.refs_4_ = bf16[1024,1280]{1,0:T(8,128)(2,1)} collective-permute-done((bf16[1024,1280]{1,0:T(8,128)(2,1)}, bf16[1024,1280]{1,0:T(8,128)(2,1)}, u32[]{:S(2)}, u32[]{:S(2)}) %collective-permute-start.4) | collective-permute-done | bytes 2621472 | tf_op jit(solution)/shard_map/ppermute | solution.py:295
  133.9 5.9 constant_dynamic-slice_fusion
  143.9 46.0 %shard_map.143 = (bf16[1024,1280]{1,0:T(8,128)(2,1)}, bf16[1024,1280]{1,0:T(8,128)(2,1)}, bf16[1024,1280]{1,0:T(8,128)(2,1)}, bf16[1024,1280]{1,0:T(8,128)(2,1)}, f32[1,1280]{1,0:T(1,128)}) custom-call(s32[2]{0:T(128)} %pad_add_fusion.idx_ref, bf16[1024,1280]{1,0:T(8,128)(2,1)} %fusion.8.refs_0_, bf16[1024,1280]{1,0:T(8,128)(2,1)} %collective-permute-done.refs_1_, ...), custom_call_target="tpu_custom_call" | custom-call | flops 26843545600 | bytes 16777216 | tf_op jit(solution)/shard_map/pallas_call | solution.py:118
  189.8 101.3 %collective-permute-done.11.refs_7_.refs_5_.refs_11_ = bf16[640,1280]{1,0:T(8,128)(2,1)} collective-permute-done((bf16[640,1280]{1,0:T(8,128)(2,1)}, bf16[640,1280]{1,0:T(8,128)(2,1)}, u32[]{:S(2)}, u32[]{:S(2)}) %collective-permute-start.11) | collective-permute-done | bytes 1638432 | tf_op jit(solution)/shard_map/ppermute | solution.py:298
  291.5 34.7 %collective-permute-done.13.refs_6_.refs_8_.refs_13_ = bf16[1280,640]{1,0:T(8,128)(2,1)} collective-permute-done((bf16[1280,640]{1,0:T(8,128)(2,1)}, bf16[1280,640]{1,0:T(8,128)(2,1)}, u32[]{:S(2)}, u32[]{:S(2)}) %collective-permute-start.13) | collective-permute-done | bytes 1638432 | tf_op jit(solution)/shard_map/ppermute | solution.py:298
  326.3 29.2 %shard_map.144 = (bf16[1024,1280]{1,0:T(8,128)(2,1)}, f32[1024,1280]{1,0:T(8,128)}, bf16[1024,1280]{1,0:T(8,128)(2,1)}, f32[1024,1280]{1,0:T(8,128)}) custom-call(s32[2]{0:T(128)} %pad_add_fusion.idx_ref, bf16[1024,1280]{1,0:T(8,128)(2,1)} %fusion.8.refs_0_, bf16[1024,1280]{1,0:T(8,128)(2,1)} %collective-permute-done.refs_1_, ...), custom_call_target="tpu_custom_call" | custom-call | flops 13421772800 | bytes 16777216 | tf_op jit(solution)/shard_map/pallas_call | solution.py:118
  355.5 4.9 collective-permute-done.14.refs_7_.refs_10_.refs_15_
  362.4 23.7 %shard_map.145 = (f32[1024,640]{1,0:T(8,128)}, f32[1024,640]{1,0:T(8,128)}, f32[1024,640]{1,0:T(8,128)}, f32[1024,640]{1,0:T(8,128)}) custom-call(s32[2]{0:T(128)} %pad_add_fusion.idx_ref, bf16[1024,1280]{1,0:T(8,128)(2,1)} %get-tuple-element.48.refs_0_, bf16[1024,1280]{1,0:T(8,128)(2,1)} %get-tuple-element.49.refs_1_, ...), custom_call_target="tpu_custom_call" | custom-call | flops 13421772800 | bytes 16777216 | tf_op jit(solution)/shard_map/pallas_call | solution.py:118
  386.1 10.4 %collective-permute-done.18.refs_6_.refs_9_.refs_14_ = bf16[1280,640]{1,0:T(8,128)(2,1)} collective-permute-done((bf16[1280,640]{1,0:T(8,128)(2,1)S(1)}, bf16[1280,640]{1,0:T(8,128)(2,1)}, u32[]{:S(2)}, u32[]{:S(2)}) %collective-permute-start.18) | collective-permute-done | bytes 1638432 | tf_op jit(solution)/shard_map/ppermute | solution.py:298
  397.0 33.7 %collective-permute-done.19.refs_7_.refs_11_.refs_16_ = bf16[1280,640]{1,0:T(8,128)(2,1)} collective-permute-done((bf16[1280,640]{1,0:T(8,128)(2,1)S(1)}, bf16[1280,640]{1,0:T(8,128)(2,1)}, u32[]{:S(2)}, u32[]{:S(2)}) %collective-permute-start.19) | collective-permute-done | bytes 1638432 | tf_op jit(solution)/shard_map/ppermute | solution.py:304
  431.4 23.3 %shard_map.146 = (f32[1024,640]{1,0:T(8,128)}, f32[1024,640]{1,0:T(8,128)}, f32[1024,640]{1,0:T(8,128)}, f32[1024,640]{1,0:T(8,128)}) custom-call(s32[2]{0:T(128)} %pad_add_fusion.idx_ref, bf16[1024,1280]{1,0:T(8,128)(2,1)} %get-tuple-element.48.refs_0_, bf16[1024,1280]{1,0:T(8,128)(2,1)} %get-tuple-element.49.refs_1_, ...), custom_call_target="tpu_custom_call" | custom-call | flops 13421772800 | bytes 16777216 | tf_op jit(solution)/shard_map/pallas_call | solution.py:118
  454.7 24.7 %shard_map.147 = (bf16[1024,1280]{1,0:T(8,128)(2,1)}, bf16[1024,1280]{1,0:T(8,128)(2,1)}, f32[1,1280]{1,0:T(1,128)}) custom-call(s32[2]{0:T(128)} %pad_add_fusion.idx_ref, bf16[1024,1280]{1,0:T(8,128)(2,1)} %refs_2_.3, bf16[1024,1280]{1,0:T(8,128)(2,1)} %collective-permute-done.1.refs_3_.refs_1_, f32[1024,1280]{1,0:T(8,128)} %get-tuple-element.61.refs_2_, ...), custom_call_target="tpu_custom_call" | custom-call | flops 13421772800 | bytes 16777216 | tf_op jit(solution)/shard_map/pallas_call | solution.py:118
  480.2 23.6 %shard_map.149 = (f32[1024,640]{1,0:T(8,128)}, f32[1024,640]{1,0:T(8,128)}, f32[1024,640]{1,0:T(8,128)}, f32[1024,640]{1,0:T(8,128)}) custom-call(s32[2]{0:T(128)} %pad_add_fusion.idx_ref, bf16[1024,1280]{1,0:T(8,128)(2,1)} %get-tuple-element.60.refs_0_.refs_4_, bf16[1024,1280]{1,0:T(8,128)(2,1)} %get-tuple-element.63.refs_1_.refs_4_, ...), custom_call_target="tpu_custom_call" | custom-call | flops 13421772800 | bytes 16777216 | tf_op jit(solution)/shard_map/pallas_call | solution.py:118
  503.8 23.5 %shard_map.148 = (f32[1024,640]{1,0:T(8,128)}, f32[1024,640]{1,0:T(8,128)}, f32[1024,640]{1,0:T(8,128)}, f32[1024,640]{1,0:T(8,128)}) custom-call(s32[2]{0:T(128)} %pad_add_fusion.idx_ref, bf16[1024,1280]{1,0:T(8,128)(2,1)} %get-tuple-element.60.refs_0_.refs_4_, bf16[1024,1280]{1,0:T(8,128)(2,1)} %get-tuple-element.63.refs_1_.refs_4_, ...), custom_call_target="tpu_custom_call" | custom-call | flops 13421772800 | bytes 16777216 | tf_op jit(solution)/shard_map/pallas_call | solution.py:118
  528.3 42.9 %shard_map.150 = (bf16[1024,1280]{1,0:T(8,128)(2,1)}, bf16[1024,1280]{1,0:T(8,128)(2,1)}, bf16[1024,1280]{1,0:T(8,128)(2,1)}, bf16[1024,1280]{1,0:T(8,128)(2,1)}) custom-call(s32[2]{0:T(128)} %pad_add_fusion.idx_ref, bf16[1024,1280]{1,0:T(8,128)(2,1)} %collective-permute-done.29.refs_0_, bf16[1024,1280]{1,0:T(8,128)(2,1)} %collective-permute-done.30.refs_1_, ...), custom_call_target="tpu_custom_call" | custom-call | flops 26843545600 | bytes 16777216 | tf_op jit(solution)/shard_map/pallas_call | solution.py:118
  571.3 14.1 %shard_map.153.refs_9_ = f32[1280,1280]{1,0:T(8,128)} custom-call(s32[2]{0:T(128)} %pad_add_fusion.idx_ref, bf16[1024,1280]{1,0:T(8,128)(2,1)} %fusion.8.refs_0_, bf16[1024,1280]{1,0:T(8,128)(2,1)} %collective-permute-done.refs_1_, bf16[1024,1280]{1,0:T(8,128)(2,1)} %collective-permute-done.2.refs_4_.refs_2_, ...), custom_call_target="tpu_custom_call" | custom-call | flops 6710886400 | bytes 16777216 | tf_op jit(solution)/shard_map/pallas_call | solution.py:273
  585.4 22.2 %shard_map.155 = (f32[1280,1280]{1,0:T(8,128)}, f32[1280,1280]{1,0:T(8,128)}) custom-call(s32[2]{0:T(128)} %pad_add_fusion.idx_ref, bf16[1024,1280]{1,0:T(8,128)(2,1)} %get-tuple-element.48.refs_0_, bf16[1024,1280]{1,0:T(8,128)(2,1)} %get-tuple-element.50.refs_2_.refs_1_, bf16[1024,1280]{1,0:T(8,128)(2,1)} %refs_2_.3, ...), custom_call_target="tpu_custom_call" | custom-call | flops 13421772800 | bytes 16777216 | tf_op jit(solution)/shard_map/pallas_call | solution.py:273
  607.5 14.2 %shard_map.152.refs_8_ = f32[1280,1280]{1,0:T(8,128)} custom-call(s32[2]{0:T(128)} %pad_add_fusion.idx_ref, bf16[1024,1280]{1,0:T(8,128)(2,1)} %fusion.8.refs_0_, bf16[1024,1280]{1,0:T(8,128)(2,1)} %collective-permute-done.refs_1_, bf16[1024,1280]{1,0:T(8,128)(2,1)} %collective-permute-done.2.refs_4_.refs_2_, ...), custom_call_target="tpu_custom_call" | custom-call | flops 6710886400 | bytes 16777216 | tf_op jit(solution)/shard_map/pallas_call | solution.py:273
  624.3 43.3 %shard_map.151 = (bf16[1024,1280]{1,0:T(8,128)(2,1)}, bf16[1024,1280]{1,0:T(8,128)(2,1)}, bf16[1024,1280]{1,0:T(8,128)(2,1)}, bf16[1024,1280]{1,0:T(8,128)(2,1)}) custom-call(s32[2]{0:T(128)} %pad_add_fusion.idx_ref, bf16[1024,1280]{1,0:T(8,128)(2,1)} %collective-permute-done.31.refs_0_.refs_2_, bf16[1024,1280]{1,0:T(8,128)(2,1)} %collective-permute-done.32.refs_1_.refs_3_, ...), custom_call_target="tpu_custom_call" | custom-call | flops 26843545600 | bytes 16777216 | tf_op jit(solution)/shard_map/pallas_call | solution.py:118
  668.0 4.4 add.150
  677.5 22.6 %shard_map.156 = (bf16[1280,1280]{1,0:T(8,128)(2,1)}, bf16[1280,1280]{1,0:T(8,128)(2,1)}) custom-call(s32[2]{0:T(128)} %pad_add_fusion.idx_ref, bf16[1024,1280]{1,0:T(8,128)(2,1)} %get-tuple-element.82.refs_0_, bf16[1024,1280]{1,0:T(8,128)(2,1)} %get-tuple-element.83.refs_1_, bf16[1024,1280]{1,0:T(8,128)(2,1)} %collective-permute-done.33.refs_2_, ...), custom_call_target="tpu_custom_call" | custom-call | flops 13421772800 | bytes 16777216 | tf_op jit(solution)/shard_map/pallas_call | solution.py:273
  700.6 22.6 %shard_map.154 = (bf16[1280,1280]{1,0:T(8,128)(2,1)}, bf16[1280,1280]{1,0:T(8,128)(2,1)}) custom-call(s32[2]{0:T(128)} %pad_add_fusion.idx_ref, bf16[1024,1280]{1,0:T(8,128)(2,1)} %collective-permute-done.29.refs_0_, bf16[1024,1280]{1,0:T(8,128)(2,1)} %collective-permute-done.30.refs_1_, bf16[1024,1280]{1,0:T(8,128)(2,1)} %collective-permute-done.31.refs_0_.refs_2_, ...), custom_call_target="tpu_custom_call" | custom-call | flops 13421772800 | bytes 16777216 | tf_op jit(solution)/shard_map/pallas_call | solution.py:273
  747.5 41.1 %collective-permute-done.22 = f32[1024,640]{1,0:T(8,128)} collective-permute-done((f32[1024,640]{1,0:T(8,128)}, f32[1024,640]{1,0:T(8,128)}, u32[]{:S(2)}, u32[]{:S(2)}) %collective-permute-start.22) | collective-permute-done | bytes 2621472 | tf_op jit(solution)/shard_map/ppermute | solution.py:295
  792.3 52.4 %collective-permute-done.28 = f32[1024,640]{1,0:T(8,128)S(1)} collective-permute-done((f32[1024,640]{1,0:T(8,128)S(1)}, f32[1024,640]{1,0:T(8,128)S(1)}, u32[]{:S(2)}, u32[]{:S(2)}) %collective-permute-start.28) | collective-permute-done | bytes 2621472 | tf_op jit(solution)/shard_map/ppermute | solution.py:295
  845.1 55.1 %collective-permute-done.25 = f32[1024,640]{1,0:T(8,128)} collective-permute-done((f32[1024,640]{1,0:T(8,128)}, f32[1024,640]{1,0:T(8,128)}, u32[]{:S(2)}, u32[]{:S(2)}) %collective-permute-start.25) | collective-permute-done | bytes 2621472 | tf_op jit(solution)/shard_map/ppermute | solution.py:295
  903.5 4.1 fusion.12
  910.1 8.5 fusion.17
  930.1 3.8 constant_dynamic-update-slice_fusion
  (185 shorter events, 83.2 us)
Async XLA Ops:
  16.0 101.0 %collective-permute-start.2 = (bf16[1024,1280]{1,0:T(8,128)(2,1)}, bf16[1024,1280]{1,0:T(8,128)(2,1)}, u32[]{:S(2)}, u32[]{:S(2)}) collective-permute-start(bf16[1024,1280]{1,0:T(8,128)(2,1)} %fusion.8.refs_0_), channel_id=1, source_target_pairs={{0,2},{2,0},{1,3},{3,1},{4,6},{6,4},{5,7},{7,5}} | collective-permute-start | bytes 7864328 | tf_op jit(solution)/shard_map/ppermute | solution.py:295
  17.5 113.9 %collective-permute-start.4 = (bf16[1024,1280]{1,0:T(8,128)(2,1)}, bf16[1024,1280]{1,0:T(8,128)(2,1)}, u32[]{:S(2)}, u32[]{:S(2)}) collective-permute-start(bf16[1024,1280]{1,0:T(8,128)(2,1)} %refs_2_.3), channel_id=1, source_target_pairs={{0,2},{2,0},{1,3},{3,1},{4,6},{6,4},{5,7},{7,5}} | collective-permute-start | bytes 7864328 | tf_op jit(solution)/shard_map/ppermute | solution.py:295
  18.0 63.7 %collective-permute-start.8 = (bf16[640,1280]{1,0:T(8,128)(2,1)}, bf16[640,1280]{1,0:T(8,128)(2,1)}, u32[]{:S(2)}, u32[]{:S(2)}) collective-permute-start(bf16[640,1280]{1,0:T(8,128)(2,1)} %get-tuple-element.104), channel_id=1, source_target_pairs={{0,5},{1,4},{4,1},{5,0},{2,7},{3,6},{6,3},{7,2}} | collective-permute-start | bytes 4915208 | tf_op jit(solution)/shard_map/ppermute | solution.py:304
  46.6 70.4 %collective-permute-start.7 = (bf16[640,1280]{1,0:T(8,128)(2,1)}, bf16[640,1280]{1,0:T(8,128)(2,1)}, u32[]{:S(2)}, u32[]{:S(2)}) collective-permute-start(bf16[640,1280]{1,0:T(8,128)(2,1)} %get-tuple-element.105), channel_id=1, source_target_pairs={{0,4},{4,0},{1,5},{5,1},{2,6},{6,2},{3,7},{7,3}} | collective-permute-start | bytes 4915208 | tf_op jit(solution)/shard_map/ppermute | solution.py:298
  49.9 91.9 %collective-permute-start.9 = (bf16[1280,1280]{1,0:T(8,128)(2,1)S(1)}, bf16[1280,1280]{1,0:T(8,128)(2,1)}, u32[]{:S(2)}, u32[]{:S(2)}) collective-permute-start(bf16[1280,1280]{1,0:T(8,128)(2,1)S(1)} %constant_dynamic-slice_fusion.3), channel_id=1, source_target_pairs={{0,1},{1,0},{2,3},{3,2},{4,5},{5,4},{6,7},{7,6}} | collective-permute-start | bytes 9830408 | tf_op jit(solution)/shard_map/ppermute | solution.py:301
  139.8 221.1 %collective-permute-start.33 = (bf16[1024,1280]{1,0:T(8,128)(2,1)}, bf16[1024,1280]{1,0:T(8,128)(2,1)}, u32[]{:S(2)}, u32[]{:S(2)}) collective-permute-start(bf16[1024,1280]{1,0:T(8,128)(2,1)} %refs_2_.3), channel_id=1, source_target_pairs={{0,4},{4,0},{1,5},{5,1},{2,6},{6,2},{3,7},{7,3}} | collective-permute-start | bytes 7864328 | tf_op jit(solution)/shard_map/ppermute | solution.py:298
  140.2 256.3 %collective-permute-start.29 = (bf16[1024,1280]{1,0:T(8,128)(2,1)}, bf16[1024,1280]{1,0:T(8,128)(2,1)}, u32[]{:S(2)}, u32[]{:S(2)}) collective-permute-start(bf16[1024,1280]{1,0:T(8,128)(2,1)} %fusion.8.refs_0_), channel_id=1, source_target_pairs={{0,4},{4,0},{1,5},{5,1},{2,6},{6,2},{3,7},{7,3}} | collective-permute-start | bytes 7864328 | tf_op jit(solution)/shard_map/ppermute | solution.py:298
  141.8 149.3 %collective-permute-start.11 = (bf16[640,1280]{1,0:T(8,128)(2,1)}, bf16[640,1280]{1,0:T(8,128)(2,1)}, u32[]{:S(2)}, u32[]{:S(2)}) collective-permute-start(bf16[640,1280]{1,0:T(8,128)(2,1)} %get-tuple-element.103), channel_id=1, source_target_pairs={{0,4},{4,0},{1,5},{5,1},{2,6},{6,2},{3,7},{7,3}} | collective-permute-start | bytes 4915208 | tf_op jit(solution)/shard_map/ppermute | solution.py:298
  142.2 184.1 %collective-permute-start.13 = (bf16[1280,640]{1,0:T(8,128)(2,1)}, bf16[1280,640]{1,0:T(8,128)(2,1)}, u32[]{:S(2)}, u32[]{:S(2)}) collective-permute-start(bf16[1280,640]{1,0:T(8,128)(2,1)} %get-tuple-element.101), channel_id=1, source_target_pairs={{0,4},{4,0},{1,5},{5,1},{2,6},{6,2},{3,7},{7,3}} | collective-permute-start | bytes 4915208 | tf_op jit(solution)/shard_map/ppermute | solution.py:298
  143.9 216.6 %collective-permute-start.14 = (bf16[1280,640]{1,0:T(8,128)(2,1)}, bf16[1280,640]{1,0:T(8,128)(2,1)}, u32[]{:S(2)}, u32[]{:S(2)}) collective-permute-start(bf16[1280,640]{1,0:T(8,128)(2,1)} %get-tuple-element.99), channel_id=1, source_target_pairs={{0,5},{1,4},{4,1},{5,0},{2,7},{3,6},{6,3},{7,2}} | collective-permute-start | bytes 4915208 | tf_op jit(solution)/shard_map/ppermute | solution.py:304
  291.1 105.3 %collective-permute-start.18 = (bf16[1280,640]{1,0:T(8,128)(2,1)S(1)}, bf16[1280,640]{1,0:T(8,128)(2,1)}, u32[]{:S(2)}, u32[]{:S(2)}) collective-permute-start(bf16[1280,640]{1,0:T(8,128)(2,1)S(1)} %copy-done.16), channel_id=1, source_target_pairs={{0,4},{4,0},{1,5},{5,1},{2,6},{6,2},{3,7},{7,3}} | collective-permute-start | bytes 4915208 | tf_op jit(solution)/shard_map/ppermute | solution.py:298
  326.3 104.4 %collective-permute-start.19 = (bf16[1280,640]{1,0:T(8,128)(2,1)S(1)}, bf16[1280,640]{1,0:T(8,128)(2,1)}, u32[]{:S(2)}, u32[]{:S(2)}) collective-permute-start(bf16[1280,640]{1,0:T(8,128)(2,1)S(1)} %copy-done.15), channel_id=1, source_target_pairs={{0,5},{1,4},{4,1},{5,0},{2,7},{3,6},{6,3},{7,2}} | collective-permute-start | bytes 4915208 | tf_op jit(solution)/shard_map/ppermute | solution.py:304
  360.4 166.9 %collective-permute-start.31 = (bf16[1024,1280]{1,0:T(8,128)(2,1)}, bf16[1024,1280]{1,0:T(8,128)(2,1)}, u32[]{:S(2)}, u32[]{:S(2)}) collective-permute-start(bf16[1024,1280]{1,0:T(8,128)(2,1)} %collective-permute-done.2.refs_4_.refs_2_), channel_id=1, source_target_pairs={{0,4},{4,0},{1,5},{5,1},{2,6},{6,2},{3,7},{7,3}} | collective-permute-start | bytes 7864328 | tf_op jit(solution)/shard_map/ppermute | solution.py:298
  360.9 166.5 %collective-permute-start.35 = (bf16[1024,1280]{1,0:T(8,128)(2,1)}, bf16[1024,1280]{1,0:T(8,128)(2,1)}, u32[]{:S(2)}, u32[]{:S(2)}) collective-permute-start(bf16[1024,1280]{1,0:T(8,128)(2,1)} %collective-permute-done.33.refs_2_), channel_id=1, source_target_pairs={{0,2},{2,0},{1,3},{3,1},{4,6},{6,4},{5,7},{7,5}} | collective-permute-start | bytes 7864328 | tf_op jit(solution)/shard_map/ppermute | solution.py:295
  396.5 131.5 %collective-permute-start.34 = (bf16[1024,1280]{1,0:T(8,128)(2,1)}, bf16[1024,1280]{1,0:T(8,128)(2,1)}, u32[]{:S(2)}, u32[]{:S(2)}) collective-permute-start(bf16[1024,1280]{1,0:T(8,128)(2,1)} %collective-permute-done.33.refs_2_), channel_id=1, source_target_pairs={{0,1},{1,0},{2,3},{3,2},{4,5},{5,4},{6,7},{7,6}} | collective-permute-start | bytes 7864328 | tf_op jit(solution)/shard_map/ppermute | solution.py:301
  396.5 131.3 %collective-permute-start.30 = (bf16[1024,1280]{1,0:T(8,128)(2,1)}, bf16[1024,1280]{1,0:T(8,128)(2,1)}, u32[]{:S(2)}, u32[]{:S(2)}) collective-permute-start(bf16[1024,1280]{1,0:T(8,128)(2,1)} %collective-permute-done.29.refs_0_), channel_id=1, source_target_pairs={{0,1},{1,0},{2,3},{3,2},{4,5},{5,4},{6,7},{7,6}} | collective-permute-start | bytes 7864328 | tf_op jit(solution)/shard_map/ppermute | solution.py:301
  430.7 237.0 %collective-permute-start.16 = (f32[1024,640]{1,0:T(8,128)}, f32[1024,640]{1,0:T(8,128)}, u32[]{:S(2)}, u32[]{:S(2)}) collective-permute-start(f32[1024,640]{1,0:T(8,128)} %get-tuple-element.55), channel_id=1, source_target_pairs={{0,1},{1,0},{2,3},{3,2},{4,5},{5,4},{6,7},{7,6}} | collective-permute-start | bytes 7864328 | tf_op jit(solution)/shard_map/ppermute | solution.py:301
  527.4 202.7 %collective-permute-start.15 = (f32[1024,640]{1,0:T(8,128)}, f32[1024,640]{1,0:T(8,128)S(1)}, u32[]{:S(2)}, u32[]{:S(2)}) collective-permute-start(f32[1024,640]{1,0:T(8,128)} %get-tuple-element.53), channel_id=1, source_target_pairs={{0,1},{1,0},{2,3},{3,2},{4,5},{5,4},{6,7},{7,6}} | collective-permute-start | bytes 7864328 | tf_op jit(solution)/shard_map/ppermute | solution.py:301
  527.4 94.3 %collective-permute-start.39 = (f32[2,1280]{1,0:T(2,128)S(1)}, f32[2,1280]{1,0:T(2,128)S(1)}, u32[]{:S(2)}, u32[]{:S(2)}) collective-permute-start(f32[2,1280]{1,0:T(2,128)S(1)} %pad_maximum_fusion), channel_id=1, source_target_pairs={{0,4},{4,0},{1,5},{5,1},{2,6},{6,2},{3,7},{7,3}} | collective-permute-start | bytes 30728 | tf_op jit(solution)/shard_map/ppermute | solution.py:298
  527.8 96.0 %collective-permute-start.32 = (bf16[1024,1280]{1,0:T(8,128)(2,1)}, bf16[1024,1280]{1,0:T(8,128)(2,1)}, u32[]{:S(2)}, u32[]{:S(2)}) collective-permute-start(bf16[1024,1280]{1,0:T(8,128)(2,1)} %collective-permute-done.31.refs_0_.refs_2_), channel_id=1, source_target_pairs={{0,1},{1,0},{2,3},{3,2},{4,5},{5,4},{6,7},{7,6}} | collective-permute-start | bytes 7864328 | tf_op jit(solution)/shard_map/ppermute | solution.py:301
  528.0 96.2 %collective-permute-start.36 = (bf16[1024,1280]{1,0:T(8,128)(2,1)}, bf16[1024,1280]{1,0:T(8,128)(2,1)}, u32[]{:S(2)}, u32[]{:S(2)}) collective-permute-start(bf16[1024,1280]{1,0:T(8,128)(2,1)} %collective-permute-done.35.refs_2_.refs_4_), channel_id=1, source_target_pairs={{0,1},{1,0},{2,3},{3,2},{4,5},{5,4},{6,7},{7,6}} | collective-permute-start | bytes 7864328 | tf_op jit(solution)/shard_map/ppermute | solution.py:301
  623.8 76.3 %collective-permute-start.27 = (f32[1024,640]{1,0:T(8,128)}, f32[1024,640]{1,0:T(8,128)}, u32[]{:S(2)}, u32[]{:S(2)}) collective-permute-start(f32[1024,640]{1,0:T(8,128)} %get-tuple-element.73), channel_id=1, source_target_pairs={{0,1},{1,0},{2,3},{3,2},{4,5},{5,4},{6,7},{7,6}} | collective-permute-start | bytes 7864328 | tf_op jit(solution)/shard_map/ppermute | solution.py:301
  624.2 102.0 %collective-permute-start.24 = (f32[1024,640]{1,0:T(8,128)}, f32[1024,640]{1,0:T(8,128)}, u32[]{:S(2)}, u32[]{:S(2)}) collective-permute-start(f32[1024,640]{1,0:T(8,128)} %get-tuple-element.69), channel_id=1, source_target_pairs={{0,1},{1,0},{2,3},{3,2},{4,5},{5,4},{6,7},{7,6}} | collective-permute-start | bytes 7864328 | tf_op jit(solution)/shard_map/ppermute | solution.py:301
  667.6 67.5 %collective-permute-start.20 = (f32[1024,640]{1,0:T(8,128)}, f32[1024,640]{1,0:T(8,128)}, u32[]{:S(2)}, u32[]{:S(2)}) collective-permute-start(f32[1024,640]{1,0:T(8,128)} %get-tuple-element.57), channel_id=1, source_target_pairs={{0,1},{1,0},{2,3},{3,2},{4,5},{5,4},{6,7},{7,6}} | collective-permute-start | bytes 7864328 | tf_op jit(solution)/shard_map/ppermute | solution.py:301
  700.2 88.5 %collective-permute-start.22 = (f32[1024,640]{1,0:T(8,128)}, f32[1024,640]{1,0:T(8,128)}, u32[]{:S(2)}, u32[]{:S(2)}) collective-permute-start(f32[1024,640]{1,0:T(8,128)} %add.153), channel_id=1, source_target_pairs={{0,2},{2,0},{1,3},{3,1},{4,6},{6,4},{5,7},{7,5}} | collective-permute-start | bytes 7864328 | tf_op jit(solution)/shard_map/ppermute | solution.py:295
  726.2 65.6 %collective-permute-start.26 = (f32[1024,640]{1,0:T(8,128)}, f32[1024,640]{1,0:T(8,128)S(1)}, u32[]{:S(2)}, u32[]{:S(2)}) collective-permute-start(f32[1024,640]{1,0:T(8,128)} %get-tuple-element.71), channel_id=1, source_target_pairs={{0,1},{1,0},{2,3},{3,2},{4,5},{5,4},{6,7},{7,6}} | collective-permute-start | bytes 7864328 | tf_op jit(solution)/shard_map/ppermute | solution.py:301
  730.1 114.6 %collective-permute-start.28 = (f32[1024,640]{1,0:T(8,128)S(1)}, f32[1024,640]{1,0:T(8,128)S(1)}, u32[]{:S(2)}, u32[]{:S(2)}) collective-permute-start(f32[1024,640]{1,0:T(8,128)S(1)} %add.162), channel_id=1, source_target_pairs={{0,2},{2,0},{1,3},{3,1},{4,6},{6,4},{5,7},{7,5}} | collective-permute-start | bytes 7864328 | tf_op jit(solution)/shard_map/ppermute | solution.py:295
  735.2 110.0 %collective-permute-start.23 = (f32[1024,640]{1,0:T(8,128)}, f32[1024,640]{1,0:T(8,128)}, u32[]{:S(2)}, u32[]{:S(2)}) collective-permute-start(f32[1024,640]{1,0:T(8,128)} %get-tuple-element.67), channel_id=1, source_target_pairs={{0,1},{1,0},{2,3},{3,2},{4,5},{5,4},{6,7},{7,6}} | collective-permute-start | bytes 7864328 | tf_op jit(solution)/shard_map/ppermute | solution.py:301
  735.2 165.0 %collective-permute-start.25 = (f32[1024,640]{1,0:T(8,128)}, f32[1024,640]{1,0:T(8,128)}, u32[]{:S(2)}, u32[]{:S(2)}) collective-permute-start(f32[1024,640]{1,0:T(8,128)} %add.159), channel_id=1, source_target_pairs={{0,2},{2,0},{1,3},{3,1},{4,6},{6,4},{5,7},{7,5}} | collective-permute-start | bytes 7864328 | tf_op jit(solution)/shard_map/ppermute | solution.py:295
  788.6 141.4 %collective-permute-start.41 = (bf16[1280,1280]{1,0:T(8,128)(2,1)}, bf16[1280,1280]{1,0:T(8,128)(2,1)}, u32[]{:S(2)}, u32[]{:S(2)}) collective-permute-start(bf16[1280,1280]{1,0:T(8,128)(2,1)} %get-tuple-element.87), channel_id=1, source_target_pairs={{0,1},{1,0},{2,3},{3,2},{4,5},{5,4},{6,7},{7,6}} | collective-permute-start | bytes 9830408 | tf_op jit(solution)/shard_map/ppermute | solution.py:301
  791.8 129.0 %collective-permute-start.37 = (bf16[640,1280]{1,0:T(8,128)(2,1)}, bf16[640,1280]{1,0:T(8,128)(2,1)}, u32[]{:S(2)}, u32[]{:S(2)}) collective-permute-start(bf16[640,1280]{1,0:T(8,128)(2,1)} %get-tuple-element.111), channel_id=1, source_target_pairs={{0,1},{1,0},{2,3},{3,2},{4,5},{5,4},{6,7},{7,6}} | collective-permute-start | bytes 4915208 | tf_op jit(solution)/shard_map/ppermute | solution.py:301
  844.7 81.4 %collective-permute-start.38 = (bf16[640,1280]{1,0:T(8,128)(2,1)}, bf16[640,1280]{1,0:T(8,128)(2,1)}, u32[]{:S(2)}, u32[]{:S(2)}) collective-permute-start(bf16[640,1280]{1,0:T(8,128)(2,1)} %get-tuple-element.109), channel_id=1, source_target_pairs={{0,1},{1,0},{2,3},{3,2},{4,5},{5,4},{6,7},{7,6}} | collective-permute-start | bytes 4915208 | tf_op jit(solution)/shard_map/ppermute | solution.py:301
  (44 other events, 1204.5 us)

commit v2 on v1

v2 whole, which is shorter than its diff:
```python
import functools
import jax
import jax.numpy as jnp
from jax import lax
from jax.experimental import pallas as pl
from jax.experimental.pallas import tpu as pltpu
from jax.sharding import PartitionSpec as P

LN_EPS = 1e-5
GELU_K = 0.7978845608028654
GELU_C = 0.044715
SWAP = [(0, 1), (1, 0)]
CROSS = [(0, 3), (1, 2), (2, 1), (3, 0)]
f32 = jnp.float32
bf16 = jnp.bfloat16
VMEM_LIMIT = 60 * 1024 * 1024
CH_ACT = 256
CH_BACK = 640
CH_GRAD = 256


def gelu_both(c):
    sq = c * c
    t = jnp.tanh(c * (GELU_K + (GELU_K * GELU_C) * sq))
    half = 0.5 * c
    h = half + half * t
    s = (0.5 + 0.5 * t) + half * (1.0 - t * t) * (GELU_K + (3.0 * GELU_K * GELU_C) * sq)
    return h, s


def mm(a, b):
    return lax.dot_general(a, b, (((1,), (0,)), ((), ())), preferred_element_type=f32)


def mmt(a, b):
    return lax.dot_general(a, b, (((1,), (1,)), ((), ())), preferred_element_type=f32)


def side(u, v):
    return jnp.concatenate([u[...], v[...]], axis=1)


def copies_of(stages, sems):
    at, out = 0, []
    for stage in stages:
        out.append([pltpu.make_async_copy(s, d, sems.at[at + i]) for i, (s, d) in enumerate(stage)])
        at += len(stage)
    return out


def tile_map(b, nb, i, *_):
    return (jnp.clip(i - b * nb, 0, nb - 1), 0)


HBM = pl.BlockSpec(memory_space=pl.ANY)


def tiled_call(body, idx, pieces, flat, weights, consts, flat_out, part_out, sums_out, scratch, bm, flops):
    nblk = len(pieces)
    n = (flat[0] if flat else pieces[0][0]).shape[0] // (nblk if flat else 1)
    nb = n // bm
    ins, in_specs, outs, out_specs = [], [], [], []
    for b, arrs in enumerate(pieces):
        for a in arrs:
            ins.append(a)
            in_specs.append(pl.BlockSpec((bm, a.shape[1]), functools.partial(tile_map, b, nb)))
    for a in flat:
        ins.append(a)
        in_specs.append(pl.BlockSpec((bm, a.shape[1]), lambda i, *_: (i, 0)))
    for w in weights:
        ins.append(w)
        in_specs.append(HBM)
    for c in consts:
        ins.append(c)
        in_specs.append(pl.BlockSpec(c.shape, lambda i, *_: (0, 0)))
    for shp in flat_out:
        outs.append(jax.ShapeDtypeStruct((n * nblk, shp[0]), shp[1]))
        out_specs.append(pl.BlockSpec((bm, shp[0]), lambda i, *_: (i, 0)))
    for width in part_out:
        for b in range(nblk):
            outs.append(jax.ShapeDtypeStruct((n, width), f32))
            out_specs.append(pl.BlockSpec((bm, width), functools.partial(tile_map, b, nb)))
    for shp in sums_out:
        outs.append(jax.ShapeDtypeStruct(shp, f32))
        out_specs.append(pl.BlockSpec(shp, lambda i, *_: (0, 0)))
    na = len(pieces[0])

    def kernel(idx_ref, *refs):
        i = pl.program_id(0)
        at = na * nblk
        fl = refs[at:at + len(flat)]
        tin = [refs[b * na:(b + 1) * na] + fl for b in range(nblk)]
        at += len(flat)
        wr = refs[at:at + len(weights)]
        at += len(weights)
        cr = refs[at:at + len(consts)]
        at += len(consts)
        tout = refs[at:at + len(flat_out)]
        at += len(flat_out)
        pout = refs[at:at + len(part_out) * nblk]
        at += len(part_out) * nblk
        sr = refs[at:at + len(sums_out)]
        at += len(sums_out)
        scr, sems = refs[at:-1], refs[-1]
        load, step = body

        @pl.when(i == 0)
        def _():
            for stage in copies_of(load(idx_ref[0], idx_ref[1], wr, scr), sems):
                for c in stage:
                    c.start()
            for s in sr:
                s[...] = jnp.zeros_like(s)

        def arrive(j):
            @pl.when(i == 0)
            def _():
                for c in copies_of(load(idx_ref[0], idx_ref[1], wr, scr), sems)[j]:
                    c.wait()

        for b in range(nblk):
            @pl.when(i // nb == b)
            def _(b=b):
                step(arrive if b == 0 else lambda j: None, tin[b], cr, tout + pout[b::nblk], sr, scr)

    call = pl.pallas_call(
        kernel,
        out_shape=outs,
        grid_spec=pltpu.PrefetchScalarGridSpec(
            num_scalar_prefetch=1, grid=(nblk * nb,), in_specs=in_specs, out_specs=out_specs,
            scratch_shapes=list(scratch) + [pltpu.SemaphoreType.DMA((32,))]),
        compiler_params=pltpu.CompilerParams(dimension_semantics=("arbitrary",), vmem_limit_bytes=VMEM_LIMIT),
        cost_estimate=pl.CostEstimate(flops=flops, bytes_accessed=1 << 24, transcendentals=0),
    )
    return call(idx, *ins)


def col_at(ref, start, size):
    return ref.at[:, pl.ds(pl.multiple_of(start, 128), size)]


def row_at(ref, start, size):
    return ref.at[pl.ds(pl.multiple_of(start, 8), size), :]


def act_call(mode, idx, blocks, slopes, groups, w_up, w_down, biases, bm, with_sums):
    fe = w_up.shape[1] // 4
    q = w_up.shape[0]
    dm = 4 * q
    ng = len(groups)
    has_c, has_d = "c" in mode, "d" in mode
    weights = [w_up, w_down]
    for _, p1, p2, _ in groups:
        weights += (list(p1) if has_c else []) + (list(p2) if has_d else [])

    def load(r, k, wr, scr):
        up, down = wr[0], wr[1]
        rest = list(wr[2:])
        bufs = list(scr)
        stages = []
        for own, p1, p2, _ in groups:
            copies = []
            if has_c:
                buf = bufs.pop(0)
                rr = r if own else 1 - r
                dep, row, cross = rest.pop(0), rest.pop(0), rest.pop(0)
                copies += [(col_at(up, (rr * 2 + k) * fe, fe), row_at(buf, r * q, q)),
                           (row, row_at(buf, (1 - r) * q, q)),
                           (dep, row_at(buf, 2 * q + r * q, q)),
                           (cross, row_at(buf, 2 * q + (1 - r) * q, q))]
            if has_d:
                buf = bufs.pop(0)
                if own:
                    dep = rest.pop(0)
                    copies += [(row_at(down, k * fe, fe), buf.at[:, 0:2 * q]), (dep, buf.at[:, 2 * q:4 * q])]
                else:
                    for j in range(4):
                        copies.append((rest.pop(0), buf.at[:, j * q:(j + 1) * q]))
            stages.append(copies)
        return stages

    def step(arrive, tin, cr, tout, sr, scr):
        tin, bufs = list(tin), list(scr)
        u, v = (tin.pop(0), tin.pop(0)) if has_c else (None, None)
        gu, gv = (tin.pop(0), tin.pop(0)) if has_d else (None, None)
        tout = list(tout)
        for g in range(ng):
            arrive(g)
            w1 = bufs.pop(0) if has_c else None
            w2 = bufs.pop(0) if has_d else None
            s_in = tin.pop(0) if not has_c else None
            h_out = tout.pop(0) if has_c and groups[g][3] else None
            x_out = tout.pop(0)
            for n0 in range(0, fe, CH_ACT):
                sl = slice(n0, n0 + CH_ACT)
                if has_c:
                    c = mm(side(u, v), w1[:, sl]) + cr[g][:, sl]
                    h, s = gelu_both(c)
                    if h_out is not None:
                        h_out[:, sl] = h.astype(bf16)
                else:
                    s = s_in[:, sl]
                if has_d:
                    p = mmt(side(gu, gv), w2[sl, :]) * s
                    x_out[:, sl] = p.astype(bf16)
                    if with_sums:
                        sr[g][:, sl] += jnp.sum(p, axis=0, keepdims=True)
                else:
                    x_out[:, sl] = s

    scratch = []
    for _ in range(ng):
        scratch += [pltpu.VMEM((dm, fe), bf16)] if has_c else []
        scratch += [pltpu.VMEM((fe, dm), bf16)] if has_d else []
    outs = []
    for g in range(ng):
        outs += [(fe, bf16)] if has_c and groups[g][3] else []
        outs += [(fe, bf16)] if has_d else [(fe, f32)]
    n = blocks[0][0].shape[0]
    flops = 2 * n * len(blocks) * dm * fe * ng * (int(has_c) + int(has_d))
    res = tiled_call((load, step), idx, blocks, slopes, weights, [b.reshape(1, fe) for b in biases] if has_c else [],
                     outs, [], [(1, fe)] * ng if with_sums else [], scratch, bm, flops)
    return res


def out_call(idx, lhs, acc, weights, load_fn, q, last, bm):
    depth = sum(a.shape[1] for a in lhs)

    def load(r, k, wr, scr):
        return [load_fn(r, k, wr, scr[0])]

    def step(arrive, tin, cr, tout, sr, scr):
        arrive(0)
        y = mm(jnp.concatenate([a[...] for a in tin[:len(lhs)]], axis=1), scr[0][...])
        for p in range(2):
            v = y[:, p * q:(p + 1) * q]
            tout[p][...] = v + tin[len(lhs) + p][...] if acc else v

    flops = 2 * lhs[0].shape[0] * 2 * q * depth
    return tiled_call((load, step), idx, [(), ()], list(lhs) + list(acc), weights, [], [(q, f32)] * (1 if last else 2), [q] if last else [], [],
                      [pltpu.VMEM((depth, 2 * q), bf16)], bm, flops)


def place_rows(r, q, buf):
    mine, theirs = r * 2 * q, (1 - r) * 2 * q
    return [buf.at[pl.ds(pl.multiple_of(start, 8), q), :] for start in (mine, mine + q, theirs, theirs + q)]


def first_back_call(idx, d_o, w_up, w1o, q, fe, bm):
    def load(r, k, wr, scr):
        pieces = [col_at(wr[0], (r * 2 + k) * fe, fe)] + list(wr[1:])
        return [list(zip(pieces, place_rows(r, q, scr[0])))]

    def step(arrive, tin, cr, tout, sr, scr):
        arrive(0)
        for j in range(2):
            y = mmt(tin[0][...], scr[0][2 * j * q:2 * (j + 1) * q, :])
            tout[2 * j][...] = y[:, :q]
            tout[2 * j + 1][...] = y[:, q:]

    flops = 2 * d_o.shape[0] * 4 * q * fe
    return tiled_call((load, step), idx, [(), ()], [d_o], [w_up] + list(w1o), [], [(q, f32)] * 4, [], [], [pltpu.VMEM((4 * q, fe), bf16)], bm, flops)


def back_call(idx, blocks, flat, w_up, w1n, w2n, q, fe, bm):
    dm = 4 * q

    def load(r, k, wr, scr):
        w1, w2 = scr
        first = [(p, w2.at[:, j * q:(j + 1) * q]) for j, p in enumerate(wr[4:])]
        pieces = [col_at(wr[0], ((1 - r) * 2 + k) * fe, fe)] + list(wr[1:4])
        return [first, list(zip(pieces, place_rows(r, q, w1)))]

    def step(arrive, tin, cr, tout, sr, scr):
        gu, gv, s_in = tin[:3]
        part = tin[3:]
        w1, w2 = scr
        dcn, outs = tout[0], tout[1:]
        arrive(0)
        for n0 in range(0, fe, CH_BACK):
            sl = slice(n0, n0 + CH_BACK)
            p = mmt(side(gu, gv), w2[sl, :]) * s_in[:, sl]
            dcn[:, sl] = p.astype(bf16)
            sr[0][:, sl] += jnp.sum(p, axis=0, keepdims=True)
        arrive(1)
        for j in range(2):
            y = mmt(dcn[...], w1[2 * j * q:2 * (j + 1) * q, :])
            outs[j][...] = part[2 * j][...] + y[:, :q]
            outs[2 + j][...] = part[2 * j + 1][...] + y[:, q:]

    flops = 2 * blocks[0][0].shape[0] * len(blocks) * dm * fe * 2
    return tiled_call((load, step), idx, blocks, flat, [w_up] + list(w1n) + list(w2n), [],
                      [(fe, bf16)] + [(q, f32)] * 2, [q, q], [(1, fe)], [pltpu.VMEM((dm, fe), bf16), pltpu.VMEM((fe, dm), bf16)], bm, flops)


def grad_call(idx, n, lhs, rhs, acc, out_dtype, halves):
    fe = rhs[0][0][0].shape[1]
    m = fe
    ng, nl, nblk = len(rhs), len(lhs[0]), len(lhs)
    ins, in_specs = [], []
    for parts in lhs:
        for p, b in parts:
            ins.append(p)
            if halves:
                in_specs.append(pl.BlockSpec((n, m // 2), functools.partial(lambda b, j, s: (b, s[0]), b), pipeline_mode=pl.Buffered(1)))
            else:
                in_specs.append(pl.BlockSpec((n, m), functools.partial(lambda b, j, s: (b, 0), b), pipeline_mode=pl.Buffered(1)))
    for parts in rhs:
        for p, b in parts:
            ins.append(p)
            in_specs.append(pl.BlockSpec((n, CH_GRAD), functools.partial(lambda b, j, s: (b, j), b)))
    used = [p for p in acc if p is not None]
    for p in used:
        ins.append(p)
        in_specs.append(pl.BlockSpec((m, CH_GRAD), lambda j, s: (0, j)))

    def kernel(idx_ref, *refs):
        refs = list(refs)
        lr = [refs.pop(0) for _ in range(nl * nblk)]
        rr = [[refs.pop(0) for _ in parts] for parts in rhs]
        ar = [None if p is None else refs.pop(0) for p in acc]
        outs, scr = refs[:ng], refs[ng]

        @pl.when(pl.program_id(0) == 0)
        def _():
            for b in range(nblk):
                for p in range(nl):
                    w = m // nl
                    scr[p * w:(p + 1) * w, b * n:(b + 1) * n] = lr[b * nl + p][...].T

        for g in range(ng):
            y = mm(scr[:, 0:len(rr[g]) * n], jnp.concatenate([v[...] for v in rr[g]], axis=0))
            if ar[g] is not None:
                y = y + ar[g][...]
            outs[g][...] = y.astype(out_dtype)

    return pl.pallas_call(
        kernel,
        out_shape=[jax.ShapeDtypeStruct((m, fe), out_dtype)] * ng,
        grid_spec=pltpu.PrefetchScalarGridSpec(
            num_scalar_prefetch=1, grid=(fe // CH_GRAD,), in_specs=in_specs,
            out_specs=[pl.BlockSpec((m, CH_GRAD), lambda j, s: (0, j))] * ng,
            scratch_shapes=[pltpu.VMEM((m, nblk * n), bf16)]),
        compiler_params=pltpu.CompilerParams(dimension_semantics=("arbitrary",), vmem_limit_bytes=VMEM_LIMIT),
        cost_estimate=pl.CostEstimate(flops=2 * n * m * fe * sum(len(p) for p in rhs), bytes_accessed=1 << 24, transcendentals=0),
    )(idx, *ins)


def final_grad_call(idx, n, lhs, rhs, acc, halves):
    fe = rhs[0][0][0].shape[1]
    nl, nblk, nt = len(lhs[0]), len(lhs), fe // CH_GRAD
    half = fe // 2

    def on(g, t):
        return jnp.clip(t - g * nt, 0, nt - 1)

    ins, in_specs = [], []
    for parts in lhs:
        for p, b in parts:
            ins.append(p)
            shape = (n, half) if halves else (n, fe)
            in_specs.append(pl.BlockSpec(shape, functools.partial(lambda b, t, s: (b, s[0] if halves else 0), b), pipeline_mode=pl.Buffered(1)))
    for g, parts in enumerate(rhs):
        for p, b in parts:
            ins.append(p)
            in_specs.append(pl.BlockSpec((n, CH_GRAD), functools.partial(lambda b, g, t, s: (b, on(g, t)), b, g)))
    for g, p in enumerate(acc):
        ins.append(p)
        in_specs.append(pl.BlockSpec((fe, CH_GRAD), functools.partial(lambda g, t, s: (0, on(g, t)), g)))
    if halves:
        outs = [jax.ShapeDtypeStruct((half, 4 * fe), bf16), jax.ShapeDtypeStruct((half, 2 * fe), bf16)]
        out_specs = [pl.BlockSpec((half, CH_GRAD), lambda t, s: (0, (jnp.where(t < nt, s[0], 1 - s[0]) * 2 + s[1]) * nt + t % nt)),
                     pl.BlockSpec((half, CH_GRAD), lambda t, s: (0, t))]
    else:
        outs = [jax.ShapeDtypeStruct((2 * fe, fe), bf16), jax.ShapeDtypeStruct((fe, fe), bf16)]
        out_specs = [pl.BlockSpec((fe, CH_GRAD), lambda t, s: (s[1], on(0, t))), pl.BlockSpec((fe, CH_GRAD), lambda t, s: (0, on(1, t)))]

    def kernel(idx_ref, *refs):
        refs = list(refs)
        lr = [refs.pop(0) for _ in range(nl * nblk)]
        rr = [[refs.pop(0) for _ in parts] for parts in rhs]
        ar = [refs.pop(0) for _ in acc]
        keep, send, scr = refs
        t = pl.program_id(0)

        @pl.when(t == 0)
        def _():
            for b in range(nblk):
                for p in range(nl):
                    w = fe // nl
                    scr[p * w:(p + 1) * w, b * n:(b + 1) * n] = lr[b * nl + p][...].T

        for g in range(2):
            @pl.when(t // nt == g)
            def _(g=g):
                y = mm(scr[...], jnp.concatenate([v[...] for v in rr[g]], axis=0)) + ar[g][...]
                if halves:
                    keep[...] = y[:half].astype(bf16)
                    send[...] = y[half:].astype(bf16)
                else:
                    (keep, send)[g][...] = y.astype(bf16)

    return pl.pallas_call(
        kernel,
        out_shape=outs,
        grid_spec=pltpu.PrefetchScalarGridSpec(
            num_scalar_prefetch=1, grid=(2 * nt,), in_specs=in_specs, out_specs=out_specs,
            scratch_shapes=[pltpu.VMEM((fe, nblk * n), bf16)]),
        compiler_params=pltpu.CompilerParams(dimension_semantics=("arbitrary",), vmem_limit_bytes=VMEM_LIMIT),
        cost_estimate=pl.CostEstimate(flops=4 * n * nblk * fe * fe, bytes_accessed=1 << 24, transcendentals=0),
    )(idx, *ins)


def solution(mesh):
    dep_size = mesh.shape["dep"]
    tok_spec = P(("part", "row", "col"), "dep")
    vec_dep = P("dep")
    part_dep = P(("part", "dep"))
    in_specs = (tok_spec, vec_dep, vec_dep, P(("dep", "row"), "col"), P("col"), P(("col", "row"), "dep"), vec_dep, tok_spec)
    out_specs = (tok_spec, tok_spec, P(("part", "dep", "row"), "col"), P(("part", "col")), P(("part", "col", "row"), "dep"), part_dep, part_dep, part_dep)

    def px(v):
        return lax.ppermute(v, "col", SWAP)

    def py(v):
        return lax.ppermute(v, "row", SWAP)

    def pd(v):
        return lax.ppermute(v, "dep", SWAP)

    def pyd(v):
        return lax.ppermute(v, ("row", "dep"), CROSS)

    def local_step(x_in, ln_scale, ln_shift, w_up, b_up, w_down, b_down, y_grad):
        r = lax.axis_index("row")
        k = lax.axis_index("dep")
        idx = jnp.stack([r, k]).astype(jnp.int32)
        n, dh_ = x_in.shape
        q = dh_ // 2
        fe = w_up.shape[1] // 4
        row_width = dh_ * dep_size

        def cols(rr, kk):
            return lax.dynamic_slice_in_dim(w_up, (rr * 2 + kk) * fe, fe, axis=1)

        def rows(kk):
            return lax.dynamic_slice_in_dim(w_down, kk * fe, fe, axis=0)

        def bias(rr):
            return lax.dynamic_slice_in_dim(b_up, (rr * 2 + k) * fe, fe, axis=0).astype(f32)

        gx = px(y_grad)
        own_o, own_n, snd_o, snd_n = cols(r, k), cols(1 - r, k), cols(r, 1 - k), cols(1 - r, 1 - k)
        w1o = (pd(snd_o), py(own_n), pyd(snd_n))
        w1n = (pd(snd_n), py(own_o), pyd(snd_o))
        rk, rk2 = rows(k), rows(1 - k)
        w2o = (pd(rk2),)
        own0, oth0 = py(rk[:, :q]), pyd(rk2[:, :q])
        own1, oth1 = py(rk[:, q:]), pyd(rk2[:, q:])
        w2n = (own0, own1, oth0, oth1)
        bo, bn = bias(r), bias(1 - r)

        x_float = x_in.astype(f32)
        row_stats = jnp.stack([jnp.sum(x_float, axis=1), jnp.sum(x_float * x_float, axis=1)], axis=1)
        row_stats = lax.psum(row_stats, "dep")
        mean_row = row_stats[:, 0:1] / row_width
        var_row = row_stats[:, 1:2] / row_width - mean_row * mean_row
        inv_std = lax.rsqrt(var_row + LN_EPS)
        x_hat = (x_float - mean_row) * inv_std
        a0 = (x_hat * ln_scale + ln_shift).astype(bf16)
        ax, ay = px(a0), py(a0)
        gy = py(y_grad)
        az, gz = px(ay), py(gx)

        def half(u):
            return (u, pd(u))

        A = [half(a0), half(ax), half(ay), half(az)]
        G = [half(y_grad), half(gx), half(gy), half(gz)]
        go, gn = (True, w1o, w2o, True), (False, w1n, w2n, True)

        def act(mode, blocks, slopes, groups, biases, sums):
            return act_call(mode, idx, blocks, slopes, groups, w_up, w_down, biases, 256, sums)

        def grad(*args):
            return grad_call(idx, n, *args)

        def whole(pair):
            return [(pair[0], 0), (pair[1], 0)]

        A0, A1, A2, A3 = [whole(p) for p in A]

        h_o, d_o, sum_o = act("cd", [A[0] + G[0], A[1] + G[1]], [], [go], [bo], True)
        h_n, s_n = act("c", [A[0], A[1]], [], [gn], [bn], False)
        two_o, two_g = [(d_o, 0), (d_o, 1)], [[(G[0][p], 0), (G[1][p], 0)] for p in range(2)]
        dw2 = grad([[(h_o, 0)], [(h_o, 1)]], two_g, [None, None], f32, False)
        dw1o, = grad([A0, A1], [two_o], [None], f32, True)
        gn_s = (False, w1n, w2n, False)
        hy, syo, syn = act("c", [A[2]], [], [go, gn_s], [bo, bn], False)
        hz, szo, szn = act("c", [A[3]], [], [go, gn_s], [bo, bn], False)

        def reduce_out(own, oth):
            oth_a, oth_x = oth
            send = own[n:] + pd(oth_x)
            return own[:n] + pd(oth_a) + px(send)

        def local_copies(j, kk, down, dep, buf):
            return [(down.at[pl.ds(pl.multiple_of(kk * fe, 8), fe), j * q:(j + 1) * q], buf.at[0:fe, 0:q]), (dep.at[:, j * q:(j + 1) * q], buf.at[0:fe, q:2 * q])]

        def far_copies(start, a, b, buf):
            return [(a, buf.at[start:start + fe, 0:q]), (b, buf.at[start:start + fe, q:2 * q])]

        def y_first(rr, kk, wr, buf):
            return local_copies(0, kk, wr[0], wr[1], buf) + far_copies(fe, wr[2], wr[3], buf)

        def out(*args):
            return out_call(idx, *args, 256)

        def y_finish(j, val):
            cs = slice(j * q, (j + 1) * q)
            return (x_in[:, cs].astype(f32) + val + b_down[cs].astype(f32)).astype(bf16)

        res = out([h_o, h_n], [], [w_down, w2o[0], own0, oth0], y_first, q, True)
        y0 = y_finish(0, reduce_out(res[0], res[1:]))
        y1o = out([h_o], [], [w_down, w2o[0]], lambda rr, kk, wr, buf: local_copies(1, kk, wr[0], wr[1], buf), q, False)
        res = out([h_n], y1o, [own1, oth1], lambda rr, kk, wr, buf: far_copies(0, wr[0], wr[1], buf), q, True)
        y1 = y_finish(1, reduce_out(res[0], res[1:]))
        y_out = jnp.concatenate([y0, y1], axis=1)

        da_o = first_back_call(idx, d_o, w_up, w1o, q, fe, 256)
        d_n, own_a, own_b, *oth, sum_n = back_call(idx, [G[0], G[1]], [s_n] + list(da_o), w_up, w1n, w2n, q, fe, 256)
        na = reduce_out(own_a, oth[:2])
        nb = reduce_out(own_b, oth[2:])
        norm_grad = jnp.concatenate([na, nb], axis=1)
        value = norm_grad * ln_scale
        grad_stats = jnp.stack([jnp.sum(value, axis=1), jnp.sum(value * x_hat, axis=1)], axis=1)
        grad_stats = lax.psum(grad_stats, "dep")
        dx = inv_std * (value - grad_stats[:, 0:1] / row_width - x_hat * (grad_stats[:, 1:2] / row_width))
        x_grad = (y_grad.astype(f32) + dx).astype(bf16)
        gains = jnp.stack([jnp.sum(norm_grad * x_hat, axis=0), jnp.sum(norm_grad, axis=0)])

        dw1n, = grad([A0, A1], [[(d_n, 0), (d_n, 1)]], [None], f32, True)
        fy = act("d", [G[2]], [syo, syn], [go, gn], [], False)
        fz = act("d", [G[3]], [szo, szn], [go, gn], [], False)
        far_g = [[(G[2][p], 0), (G[3][p], 0)] for p in range(2)]
        w_up_grad, send1 = final_grad_call(idx, n, [A2, A3], [[(fy[g], 0), (fz[g], 0)] for g in range(2)], [dw1o, dw1n], True)
        w_down_grad, send2 = final_grad_call(idx, n, [[(hy, 0)], [(hz, 0)]], far_g, dw2, False)
        got1, got2 = pd(send1), pd(send2)
        for g, rr in enumerate((r, 1 - r)):
            w_up_grad = lax.dynamic_update_slice_in_dim(w_up_grad, got1[:, g * fe:(g + 1) * fe], (rr * 2 + 1 - k) * fe, axis=1)
        w_down_grad = lax.dynamic_update_slice_in_dim(w_down_grad, got2, (1 - k) * fe, axis=0)

        def both(v):
            v = v + px(v)
            return v + py(v)

        b_down_grad = both(jnp.sum(y_grad.astype(f32), axis=0))
        gain_sums = both(gains)
        full = jnp.concatenate([sum_o, sum_n]) + py(jnp.concatenate([sum_n, sum_o]))
        oth = pd(full)
        b_up_grad = jnp.zeros(b_up.shape, f32)
        for v, rr, kk in ((full[0], r, k), (full[1], 1 - r, k), (oth[0], r, 1 - k), (oth[1], 1 - r, 1 - k)):
            b_up_grad = lax.dynamic_update_slice_in_dim(b_up_grad, v, (rr * 2 + kk) * fe, axis=0)
        return (y_out, x_grad, w_up_grad, b_up_grad, w_down_grad, b_down_grad, gain_sums[0], gain_sums[1])

    return jax.shard_map(local_step, mesh=mesh, in_specs=in_specs, out_specs=out_specs, check_vma=False)
```

time: 938 us -> 937 us (level)
  Pallas kernels: 376 us -> 395 us
  waiting for transfers between devices: 442 us -> 423 us
  local copies, waits for them, and re-layouts: 39.8 us -> 26.3 us
    pallas_call x0 -> x2, Pallas kernels: none -> 48.9 us  [final_grad_call(): pl.pallas_call(kernel, out_shape=outs, grid_spec=pltpu.PrefetchScalarGrid...]
    pallas_call x5 -> x3, Pallas kernels: 95.7 us -> 50.5 us  [grad_call(): pl.pallas_call(kernel, out_shape=[jax.ShapeDtypeStruct((m, fe), out_dtype...]
    ppermute x10, waiting for transfers between devices: 181 us -> 137 us  [py(): return lax.ppermute(v, 'row', SWAP)]
    ppermute x4, waiting for transfers between devices: 97.2 us -> 129 us  [pyd(): return lax.ppermute(v, ('row', 'dep'), CROSS)]
    pallas_call x9 -> x11, Pallas kernels: 280 us -> 296 us  [tiled_call(): return call(idx, *ins)]
    add x8 -> x6, other arithmetic: 23.5 us -> 23.1 us  [the longest x4 15.8 us: reduce_out(): send = own[n:] + pd(oth_x)]
  transfers between devices with their start and end apart: 46 -> 45, of which waited for: 14 -> 12; matrix products, arithmetic and copies ran while one was open for 7% -> 7% of each run, Pallas kernels for 40% -> 42%
where the time goes in v2:
time: 937 us; the launch traced here: 932 us
  waiting for transfers between devices  423 us (45%)
  Pallas kernels  395 us (42%)
  other arithmetic  47.3 us (5%)
  starting transfers between devices  33.3 us (4%)
  local copies, waits for them, and re-layouts  26.3 us (3%)
    pallas_call x11, Pallas kernels, tiled_call(): return call(idx, *ins)  296 us
    ppermute x9, waiting for transfers between devices, px(): return lax.ppermute(v, 'col', SWAP)  156 us
    ppermute x10, waiting for transfers between devices, py(): return lax.ppermute(v, 'row', SWAP)  137 us
    ppermute x4, waiting for transfers between devices, pyd(): return lax.ppermute(v, ('row', 'dep'), CROSS)  129 us
    pallas_call x3, Pallas kernels, grad_call(): pl.pallas_call(kernel, out_shape=[jax.ShapeDtypeStruct((m, fe), out_dtype...  50.5 us
    pallas_call x2, Pallas kernels, final_grad_call(): pl.pallas_call(kernel, out_shape=outs, grid_spec=pltpu.PrefetchScalarGrid...  48.9 us
  transfers between devices with their start and end apart: 45, of which 12 were waited for; matrix products, arithmetic and copies ran while one was open for 7% of the time, Pallas kernels for 42%

profile of v2, /device:TPU:0, one launch (start us, length us, event | category | flops | bytes accessed | tf_op | source)
XLA Modules:
  0.0 931.7 jit_solution(17814472072128195760)
XLA Ops:
  11.8 5.8 constant_dynamic-slice_fusion.5
  23.8 32.9 %collective-permute-done.7.refs_11_.refs_3_.refs_5_ = bf16[640,1280]{1,0:T(8,128)(2,1)} collective-permute-done((bf16[640,1280]{1,0:T(8,128)(2,1)}, bf16[640,1280]{1,0:T(8,128)(2,1)}, u32[]{:S(2)}, u32[]{:S(2)}) %collective-permute-start.7) | collective-permute-done | bytes 1638432 | tf_op jit(solution)/shard_map/ppermute | solution.py:426
  56.6 34.7 %collective-permute-done.8.refs_12_.refs_4_.refs_6_ = bf16[640,1280]{1,0:T(8,128)(2,1)} collective-permute-done((bf16[640,1280]{1,0:T(8,128)(2,1)}, bf16[640,1280]{1,0:T(8,128)(2,1)}, u32[]{:S(2)}, u32[]{:S(2)}) %collective-permute-start.8) | collective-permute-done | bytes 1638432 | tf_op jit(solution)/shard_map/ppermute | solution.py:432
  91.9 33.6 %collective-permute-done.4.refs_6_.refs_2_.refs_3_ = bf16[1024,1280]{1,0:T(8,128)(2,1)} collective-permute-done((bf16[1024,1280]{1,0:T(8,128)(2,1)}, bf16[1024,1280]{1,0:T(8,128)(2,1)}, u32[]{:S(2)}, u32[]{:S(2)}) %collective-permute-start.4) | collective-permute-done | bytes 2621472 | tf_op jit(solution)/shard_map/ppermute | solution.py:423
  128.0 5.8 constant_dynamic-slice_fusion
  138.2 42.4 %shard_map.143 = (bf16[2048,1280]{1,0:T(8,128)(2,1)}, bf16[2048,1280]{1,0:T(8,128)(2,1)}, f32[1,1280]{1,0:T(1,128)}) custom-call(s32[2]{0:T(128)} %pad_add_fusion.idx_ref, bf16[1024,1280]{1,0:T(8,128)(2,1)} %fusion.8.refs_0_, bf16[1024,1280]{1,0:T(8,128)(2,1)} %collective-permute-done.refs_1_, bf16[1024,1280]{1,0:T(8,128)(2,1)} %refs_2_.9, ...), custom_call_target="tpu_custom_call" | custom-call | flops 26843545600 | bytes 16777216 | tf_op jit(solution)/shard_map/pallas_call | solution.py:135
  182.3 82.0 %collective-permute-done.11.refs_7_.refs_11_.refs_8_ = bf16[640,1280]{1,0:T(8,128)(2,1)S(1)} collective-permute-done((bf16[640,1280]{1,0:T(8,128)(2,1)}, bf16[640,1280]{1,0:T(8,128)(2,1)S(1)}, u32[]{:S(2)}, u32[]{:S(2)}) %collective-permute-start.11) | collective-permute-done | bytes 1638432 | tf_op jit(solution)/shard_map/ppermute | solution.py:426
  265.4 22.3 %shard_map.148 = (f32[2048,640]{1,0:T(8,128)}, f32[2048,640]{1,0:T(8,128)}, f32[2048,640]{1,0:T(8,128)}, f32[2048,640]{1,0:T(8,128)}) custom-call(s32[2]{0:T(128)} %pad_add_fusion.idx_ref, bf16[2048,1280]{1,0:T(8,128)(2,1)} %get-tuple-element.60.refs_0_.refs_4_.refs_5_, bf16[640,5120]{1,0:T(8,128)(2,1)} %refs_4_.5, ...), custom_call_target="tpu_custom_call" | custom-call | flops 13421772800 | bytes 16777216 | tf_op jit(solution)/shard_map/pallas_call | solution.py:135
  289.5 10.0 %collective-permute-done.13.refs_4_.refs_13_.refs_7_ = bf16[1280,640]{1,0:T(8,128)(2,1)} collective-permute-done((bf16[1280,640]{1,0:T(8,128)(2,1)}, bf16[1280,640]{1,0:T(8,128)(2,1)}, u32[]{:S(2)}, u32[]{:S(2)}) %collective-permute-start.13) | collective-permute-done | bytes 1638432 | tf_op jit(solution)/shard_map/ppermute | solution.py:426
  300.4 27.3 %shard_map.144 = (bf16[2048,1280]{1,0:T(8,128)(2,1)}, f32[2048,1280]{1,0:T(8,128)}) custom-call(s32[2]{0:T(128)} %pad_add_fusion.idx_ref, bf16[1024,1280]{1,0:T(8,128)(2,1)} %fusion.8.refs_0_, bf16[1024,1280]{1,0:T(8,128)(2,1)} %collective-permute-done.refs_1_, bf16[1024,1280]{1,0:T(8,128)(2,1)} %copy-done.4, ...), custom_call_target="tpu_custom_call" | custom-call | flops 13421772800 | bytes 16777216 | tf_op jit(solution)/shard_map/pallas_call | solution.py:135
  328.6 61.6 %collective-permute-done.14.refs_5_.refs_15_.refs_9_ = bf16[1280,640]{1,0:T(8,128)(2,1)} collective-permute-done((bf16[1280,640]{1,0:T(8,128)(2,1)}, bf16[1280,640]{1,0:T(8,128)(2,1)}, u32[]{:S(2)}, u32[]{:S(2)}) %collective-permute-start.14) | collective-permute-done | bytes 1638432 | tf_op jit(solution)/shard_map/ppermute | solution.py:432
  392.0 21.9 %shard_map.145 = (f32[2048,640]{1,0:T(8,128)}, f32[1024,640]{1,0:T(8,128)}, f32[1024,640]{1,0:T(8,128)}) custom-call(s32[2]{0:T(128)} %pad_add_fusion.idx_ref, bf16[2048,1280]{1,0:T(8,128)(2,1)} %get-tuple-element.49.refs_0_.refs_1_, bf16[2048,1280]{1,0:T(8,128)(2,1)} %get-tuple-element.50.refs_1_.refs_0_, bf16[2560,1280]{1,0:T(8,128)(2,1)} %refs_5_.5, ...), custom_call_target="tpu_custom_call" | custom-call | flops 13421772800 | bytes 16777216 | tf_op jit(solution)/shard_map/pallas_call | solution.py:135
  413.9 12.0 %collective-permute-done.18.refs_3_.refs_14_.refs_8_ = bf16[1280,640]{1,0:T(8,128)(2,1)} collective-permute-done((bf16[1280,640]{1,0:T(8,128)(2,1)S(1)}, bf16[1280,640]{1,0:T(8,128)(2,1)}, u32[]{:S(2)}, u32[]{:S(2)}) %collective-permute-start.18) | collective-permute-done | bytes 1638432 | tf_op jit(solution)/shard_map/ppermute | solution.py:426
  427.6 32.8 %collective-permute-done.19.refs_4_.refs_16_.refs_10_ = bf16[1280,640]{1,0:T(8,128)(2,1)} collective-permute-done((bf16[1280,640]{1,0:T(8,128)(2,1)S(1)}, bf16[1280,640]{1,0:T(8,128)(2,1)}, u32[]{:S(2)}, u32[]{:S(2)}) %collective-permute-start.19) | collective-permute-done | bytes 1638432 | tf_op jit(solution)/shard_map/ppermute | solution.py:432
  460.8 43.5 %shard_map.149 = (bf16[2048,1280]{1,0:T(8,128)(2,1)}, f32[2048,640]{1,0:T(8,128)}, f32[2048,640]{1,0:T(8,128)}, f32[1024,640]{1,0:T(8,128)}, f32[1024,640]{1,0:T...) custom-call(s32[2]{0:T(128)} %pad_add_fusion.idx_ref, bf16[1024,1280]{1,0:T(8,128)(2,1)} %refs_2_.9, ...), custom_call_target="tpu_custom_call" | custom-call | flops 26843545600 | bytes 16777216 | tf_op jit(solution)/shard_map/pallas_call | solution.py:135
  504.3 21.9 %shard_map.157 = (f32[1280,1280]{1,0:T(8,128)}, f32[1280,1280]{1,0:T(8,128)}) custom-call(s32[2]{0:T(128)} %pad_add_fusion.idx_ref, bf16[2048,1280]{1,0:T(8,128)(2,1)} %get-tuple-element.49.refs_0_.refs_1_, bf16[2048,1280]{1,0:T(8,128)(2,1)} %get-tuple-element.49.refs_0_.refs_1_, bf16[1024,1280]{1,0:T(8,128)(2,1)} %refs_2_.9, ...), custom_call_target="tpu_custom_call" | custom-call | flops 13421772800 | bytes 16777216 | tf_op jit(solution)/shard_map/pallas_call | solution.py:337
  526.4 27.4 %shard_map.150 = (bf16[1024,1280]{1,0:T(8,128)(2,1)}, f32[1024,1280]{1,0:T(8,128)}, f32[1024,1280]{1,0:T(8,128)}) custom-call(s32[2]{0:T(128)} %pad_add_fusion.idx_ref, bf16[1024,1280]{1,0:T(8,128)(2,1)} %collective-permute-done.29.refs_0_, bf16[1024,1280]{1,0:T(8,128)(2,1)} %collective-permute-done.30.refs_1_, bf16[640,5120]{1,0:T(8,128)(2,1)} %refs_4_.5, ...), custom_call_target="tpu_custom_call" | custom-call | flops 13421772800 | bytes 16777216 | tf_op jit(solution)/shard_map/pallas_call | solution.py:135
  555.7 25.5 %shard_map.151 = (bf16[1024,1280]{1,0:T(8,128)(2,1)}, bf16[1024,1280]{1,0:T(8,128)(2,1)}) custom-call(s32[2]{0:T(128)} %pad_add_fusion.idx_ref, bf16[1024,1280]{1,0:T(8,128)(2,1)} %collective-permute-done.33.refs_0_.refs_2_, bf16[1024,1280]{1,0:T(8,128)(2,1)} %collective-permute-done.34.refs_1_.refs_4_, f32[1024,1280]{1,0:T(8,128)} %get-tuple-element.71.refs_2_, ...), custom_call_target="tpu_custom_call" | custom-call | flops 13421772800 | bytes 16777216 | tf_op jit(solution)/shard_map/pallas_call | solution.py:135
  581.2 15.1 %shard_map.146 = (f32[2048,640]{1,0:T(8,128)}, f32[2048,640]{1,0:T(8,128)}) custom-call(s32[2]{0:T(128)} %pad_add_fusion.idx_ref, bf16[2048,1280]{1,0:T(8,128)(2,1)} %get-tuple-element.49.refs_0_.refs_1_, bf16[2560,1280]{1,0:T(8,128)(2,1)} %refs_5_.5, bf16[1280,1280]{1,0:T(8,128)(2,1)} %collective-permute-done.9.refs_13_.refs_3_.refs_2_.refs_6_), custom_call_target="tpu_custom_call" | custom-call | flops 6710886400 | bytes 16777216 | tf_op jit(solution)/shard_map/pallas_call | solution.py:135
  596.3 14.2 %shard_map.154.refs_8_ = f32[1280,1280]{1,0:T(8,128)} custom-call(s32[2]{0:T(128)} %pad_add_fusion.idx_ref, bf16[1024,1280]{1,0:T(8,128)(2,1)} %fusion.8.refs_0_, bf16[1024,1280]{1,0:T(8,128)(2,1)} %collective-permute-done.refs_1_, bf16[1024,1280]{1,0:T(8,128)(2,1)} %copy-done.4, bf16[1024,1280]{1,0:T(8,128)(2,1)} %collective-permute-done.3.refs_5_.refs_3_, ...), custom_call_target="tpu_custom_call" | custom-call | flops 6710886400 | bytes 16777216 | tf_op jit(solution)/shard_map/pallas_call | solution.py:337
  611.0 14.4 %shard_map.155.refs_9_ = f32[1280,1280]{1,0:T(8,128)} custom-call(s32[2]{0:T(128)} %pad_add_fusion.idx_ref, bf16[1024,1280]{1,0:T(8,128)(2,1)} %fusion.8.refs_0_, bf16[1024,1280]{1,0:T(8,128)(2,1)} %collective-permute-done.refs_1_, bf16[1024,1280]{1,0:T(8,128)(2,1)} %copy-done.4, bf16[1024,1280]{1,0:T(8,128)(2,1)} %collective-permute-done.3.refs_5_.refs_3_, ...), custom_call_target="tpu_custom_call" | custom-call | flops 6710886400 | bytes 16777216 | tf_op jit(solution)/shard_map/pallas_call | solution.py:337
  625.4 17.1 %shard_map.147 = (f32[2048,640]{1,0:T(8,128)}, f32[1024,640]{1,0:T(8,128)}, f32[1024,640]{1,0:T(8,128)}) custom-call(s32[2]{0:T(128)} %pad_add_fusion.idx_ref, bf16[2048,1280]{1,0:T(8,128)(2,1)} %get-tuple-element.50.refs_1_.refs_0_, f32[2048,640]{1,0:T(8,128)} %get-tuple-element.54.refs_1_, f32[2048,640]{1,0:T(8,128)} %get-tuple-element.55.refs_2_, ...), custom_call_target="tpu_custom_call" | custom-call | flops 6710886400 | bytes 16777216 | tf_op jit(solution)/shard_map/pallas_call | solution.py:135
  648.7 4.4 slice_add_fusion
  657.1 27.2 %shard_map.152 = (bf16[1024,1280]{1,0:T(8,128)(2,1)}, f32[1024,1280]{1,0:T(8,128)}, f32[1024,1280]{1,0:T(8,128)}) custom-call(s32[2]{0:T(128)} %pad_add_fusion.idx_ref, bf16[1024,1280]{1,0:T(8,128)(2,1)} %collective-permute-done.31.refs_0_.refs_2_, bf16[1024,1280]{1,0:T(8,128)(2,1)} %collective-permute-done.32.refs_1_.refs_3_, bf16[640,5120]{1,0:T(8,128)(2,1)} %refs_4_.5, ...), custom_call_target="tpu_custom_call" | custom-call | flops 13421772800 | bytes 16777216 | tf_op jit(solution)/shard_map/pallas_call | solution.py:135
  685.8 25.8 %shard_map.153 = (bf16[1024,1280]{1,0:T(8,128)(2,1)}, bf16[1024,1280]{1,0:T(8,128)(2,1)}) custom-call(s32[2]{0:T(128)} %pad_add_fusion.idx_ref, bf16[1024,1280]{1,0:T(8,128)(2,1)} %collective-permute-done.35.refs_0_.refs_3_, bf16[1024,1280]{1,0:T(8,128)(2,1)} %collective-permute-done.36.refs_1_.refs_5_, f32[1024,1280]{1,0:T(8,128)} %get-tuple-element.74.refs_2_, ...), custom_call_target="tpu_custom_call" | custom-call | flops 13421772800 | bytes 16777216 | tf_op jit(solution)/shard_map/pallas_call | solution.py:135
  716.6 24.6 %shard_map.158 = (bf16[2560,1280]{1,0:T(8,128)(2,1)}, bf16[1280,1280]{1,0:T(8,128)(2,1)}) custom-call(s32[2]{0:T(128)} %pad_add_fusion.idx_ref, bf16[1024,1280]{1,0:T(8,128)(2,1)} %get-tuple-element.84.refs_0_, bf16[1024,1280]{1,0:T(8,128)(2,1)} %get-tuple-element.85.refs_1_, bf16[1024,1280]{1,0:T(8,128)(2,1)} %collective-permute-done.33.refs_0_.refs_2_, ...), custom_call_target="tpu_custom_call" | custom-call | flops 13421772800 | bytes 16777216 | tf_op jit(solution)/shard_map/pallas_call | solution.py:403
  741.2 24.3 %shard_map.156 = (bf16[640,5120]{1,0:T(8,128)(2,1)}, bf16[640,2560]{1,0:T(8,128)(2,1)}) custom-call(s32[2]{0:T(128)} %pad_add_fusion.idx_ref, bf16[1024,1280]{1,0:T(8,128)(2,1)} %collective-permute-done.29.refs_0_, bf16[1024,1280]{1,0:T(8,128)(2,1)} %collective-permute-done.30.refs_1_, bf16[1024,1280]{1,0:T(8,128)(2,1)} %collective-permute-done.31.refs_0_.refs_2_, ...), custom_call_target="tpu_custom_call" | custom-call | flops 13421772800 | bytes 16777216 | tf_op jit(solution)/shard_map/pallas_call | solution.py:403
  771.7 28.9 %collective-permute-done.25 = f32[1024,640]{1,0:T(8,128)} collective-permute-done((f32[1024,640]{1,0:T(8,128)}, f32[1024,640]{1,0:T(8,128)}, u32[]{:S(2)}, u32[]{:S(2)}) %collective-permute-start.25) | collective-permute-done | bytes 2621472 | tf_op jit(solution)/shard_map/ppermute | solution.py:423
  809.6 5.6 convert_reduce_fusion.1
  817.0 39.7 %collective-permute-done.17 = f32[1024,640]{1,0:T(8,128)} collective-permute-done((f32[1024,640]{1,0:T(8,128)}, f32[1024,640]{1,0:T(8,128)}, u32[]{:S(2)}, u32[]{:S(2)}) %collective-permute-start.17) | collective-permute-done | bytes 2621472 | tf_op jit(solution)/shard_map/ppermute | solution.py:423
  858.2 54.3 %collective-permute-done.22 = f32[1024,640]{1,0:T(8,128)} collective-permute-done((f32[1024,640]{1,0:T(8,128)}, f32[1024,640]{1,0:T(8,128)}, u32[]{:S(2)}, u32[]{:S(2)}) %collective-permute-start.22) | collective-permute-done | bytes 2621472 | tf_op jit(solution)/shard_map/ppermute | solution.py:423
  912.5 6.6 add_convert_fusion.1
  (176 shorter events, 84.8 us)
Async XLA Ops:
  9.0 82.7 %collective-permute-start.2 = (bf16[1024,1280]{1,0:T(8,128)(2,1)}, bf16[1024,1280]{1,0:T(8,128)(2,1)S(1)}, u32[]{:S(2)}, u32[]{:S(2)}) collective-permute-start(bf16[1024,1280]{1,0:T(8,128)(2,1)} %fusion.8.refs_0_), channel_id=1, source_target_pairs={{0,2},{2,0},{1,3},{3,1},{4,6},{6,4},{5,7},{7,5}} | collective-permute-start | bytes 7864328 | tf_op jit(solution)/shard_map/ppermute | solution.py:423
  11.8 113.7 %collective-permute-start.4 = (bf16[1024,1280]{1,0:T(8,128)(2,1)}, bf16[1024,1280]{1,0:T(8,128)(2,1)}, u32[]{:S(2)}, u32[]{:S(2)}) collective-permute-start(bf16[1024,1280]{1,0:T(8,128)(2,1)} %refs_2_.9), channel_id=1, source_target_pairs={{0,2},{2,0},{1,3},{3,1},{4,6},{6,4},{5,7},{7,5}} | collective-permute-start | bytes 7864328 | tf_op jit(solution)/shard_map/ppermute | solution.py:423
  19.7 71.7 %collective-permute-start.8 = (bf16[640,1280]{1,0:T(8,128)(2,1)}, bf16[640,1280]{1,0:T(8,128)(2,1)}, u32[]{:S(2)}, u32[]{:S(2)}) collective-permute-start(bf16[640,1280]{1,0:T(8,128)(2,1)} %get-tuple-element.108), channel_id=1, source_target_pairs={{0,5},{1,4},{4,1},{5,0},{2,7},{3,6},{6,3},{7,2}} | collective-permute-start | bytes 4915208 | tf_op jit(solution)/shard_map/ppermute | solution.py:432
  23.7 112.1 %collective-permute-start.9 = (bf16[1280,1280]{1,0:T(8,128)(2,1)}, bf16[1280,1280]{1,0:T(8,128)(2,1)}, u32[]{:S(2)}, u32[]{:S(2)}) collective-permute-start(bf16[1280,1280]{1,0:T(8,128)(2,1)} %constant_dynamic-slice_fusion.3), channel_id=1, source_target_pairs={{0,1},{1,0},{2,3},{3,2},{4,5},{5,4},{6,7},{7,6}} | collective-permute-start | bytes 9830408 | tf_op jit(solution)/shard_map/ppermute | solution.py:429
  56.6 77.2 %collective-permute-start = (bf16[1024,1280]{1,0:T(8,128)(2,1)}, bf16[1024,1280]{1,0:T(8,128)(2,1)}, u32[]{:S(2)}, u32[]{:S(2)}) collective-permute-start(bf16[1024,1280]{1,0:T(8,128)(2,1)} %fusion.8.refs_0_), channel_id=1, source_target_pairs={{0,1},{1,0},{2,3},{3,2},{4,5},{5,4},{6,7},{7,6}} | collective-permute-start | bytes 7864328 | tf_op jit(solution)/shard_map/ppermute | solution.py:429
  134.3 153.4 %collective-permute-start.12 = (bf16[640,1280]{1,0:T(8,128)(2,1)}, bf16[640,1280]{1,0:T(8,128)(2,1)}, u32[]{:S(2)}, u32[]{:S(2)}) collective-permute-start(bf16[640,1280]{1,0:T(8,128)(2,1)} %get-tuple-element.109), channel_id=1, source_target_pairs={{0,5},{1,4},{4,1},{5,0},{2,7},{3,6},{6,3},{7,2}} | collective-permute-start | bytes 4915208 | tf_op jit(solution)/shard_map/ppermute | solution.py:432
  135.8 191.9 %collective-permute-start.29 = (bf16[1024,1280]{1,0:T(8,128)(2,1)}, bf16[1024,1280]{1,0:T(8,128)(2,1)}, u32[]{:S(2)}, u32[]{:S(2)}) collective-permute-start(bf16[1024,1280]{1,0:T(8,128)(2,1)} %fusion.8.refs_0_), channel_id=1, source_target_pairs={{0,4},{4,0},{1,5},{5,1},{2,6},{6,2},{3,7},{7,3}} | collective-permute-start | bytes 7864328 | tf_op jit(solution)/shard_map/ppermute | solution.py:426
  136.1 128.1 %collective-permute-start.11 = (bf16[640,1280]{1,0:T(8,128)(2,1)}, bf16[640,1280]{1,0:T(8,128)(2,1)S(1)}, u32[]{:S(2)}, u32[]{:S(2)}) collective-permute-start(bf16[640,1280]{1,0:T(8,128)(2,1)} %get-tuple-element.107), channel_id=1, source_target_pairs={{0,4},{4,0},{1,5},{5,1},{2,6},{6,2},{3,7},{7,3}} | collective-permute-start | bytes 4915208 | tf_op jit(solution)/shard_map/ppermute | solution.py:426
  137.8 161.7 %collective-permute-start.13 = (bf16[1280,640]{1,0:T(8,128)(2,1)}, bf16[1280,640]{1,0:T(8,128)(2,1)}, u32[]{:S(2)}, u32[]{:S(2)}) collective-permute-start(bf16[1280,640]{1,0:T(8,128)(2,1)} %get-tuple-element.104), channel_id=1, source_target_pairs={{0,4},{4,0},{1,5},{5,1},{2,6},{6,2},{3,7},{7,3}} | collective-permute-start | bytes 4915208 | tf_op jit(solution)/shard_map/ppermute | solution.py:426
  180.6 246.9 %collective-permute-start.33 = (bf16[1024,1280]{1,0:T(8,128)(2,1)}, bf16[1024,1280]{1,0:T(8,128)(2,1)}, u32[]{:S(2)}, u32[]{:S(2)}) collective-permute-start(bf16[1024,1280]{1,0:T(8,128)(2,1)} %refs_2_.9), channel_id=1, source_target_pairs={{0,4},{4,0},{1,5},{5,1},{2,6},{6,2},{3,7},{7,3}} | collective-permute-start | bytes 7864328 | tf_op jit(solution)/shard_map/ppermute | solution.py:426
  264.3 125.9 %collective-permute-start.14 = (bf16[1280,640]{1,0:T(8,128)(2,1)}, bf16[1280,640]{1,0:T(8,128)(2,1)}, u32[]{:S(2)}, u32[]{:S(2)}) collective-permute-start(bf16[1280,640]{1,0:T(8,128)(2,1)} %get-tuple-element.102), channel_id=1, source_target_pairs={{0,5},{1,4},{4,1},{5,0},{2,7},{3,6},{6,3},{7,2}} | collective-permute-start | bytes 4915208 | tf_op jit(solution)/shard_map/ppermute | solution.py:432
  287.8 138.1 %collective-permute-start.18 = (bf16[1280,640]{1,0:T(8,128)(2,1)S(1)}, bf16[1280,640]{1,0:T(8,128)(2,1)}, u32[]{:S(2)}, u32[]{:S(2)}) collective-permute-start(bf16[1280,640]{1,0:T(8,128)(2,1)S(1)} %copy-done.7), channel_id=1, source_target_pairs={{0,4},{4,0},{1,5},{5,1},{2,6},{6,2},{3,7},{7,3}} | collective-permute-start | bytes 4915208 | tf_op jit(solution)/shard_map/ppermute | solution.py:426
  299.5 160.9 %collective-permute-start.19 = (bf16[1280,640]{1,0:T(8,128)(2,1)S(1)}, bf16[1280,640]{1,0:T(8,128)(2,1)}, u32[]{:S(2)}, u32[]{:S(2)}) collective-permute-start(bf16[1280,640]{1,0:T(8,128)(2,1)S(1)} %copy-done.6), channel_id=1, source_target_pairs={{0,5},{1,4},{4,1},{5,0},{2,7},{3,6},{6,3},{7,2}} | collective-permute-start | bytes 4915208 | tf_op jit(solution)/shard_map/ppermute | solution.py:432
  327.7 198.6 %collective-permute-start.30 = (bf16[1024,1280]{1,0:T(8,128)(2,1)}, bf16[1024,1280]{1,0:T(8,128)(2,1)}, u32[]{:S(2)}, u32[]{:S(2)}) collective-permute-start(bf16[1024,1280]{1,0:T(8,128)(2,1)} %collective-permute-done.29.refs_0_), channel_id=1, source_target_pairs={{0,1},{1,0},{2,3},{3,2},{4,5},{5,4},{6,7},{7,6}} | collective-permute-start | bytes 7864328 | tf_op jit(solution)/shard_map/ppermute | solution.py:429
  390.1 220.3 %collective-permute-start.31 = (bf16[1024,1280]{1,0:T(8,128)(2,1)}, bf16[1024,1280]{1,0:T(8,128)(2,1)}, u32[]{:S(2)}, u32[]{:S(2)}) collective-permute-start(bf16[1024,1280]{1,0:T(8,128)(2,1)} %collective-permute-done.29.refs_0_), channel_id=1, source_target_pairs={{0,2},{2,0},{1,3},{3,1},{4,6},{6,4},{5,7},{7,5}} | collective-permute-start | bytes 7864328 | tf_op jit(solution)/shard_map/ppermute | solution.py:423
  425.9 216.6 %collective-permute-start.35 = (bf16[1024,1280]{1,0:T(8,128)(2,1)}, bf16[1024,1280]{1,0:T(8,128)(2,1)}, u32[]{:S(2)}, u32[]{:S(2)}) collective-permute-start(bf16[1024,1280]{1,0:T(8,128)(2,1)} %collective-permute-done.4.refs_6_.refs_2_.refs_3_), channel_id=1, source_target_pairs={{0,4},{4,0},{1,5},{5,1},{2,6},{6,2},{3,7},{7,3}} | collective-permute-start | bytes 7864328 | tf_op jit(solution)/shard_map/ppermute | solution.py:426
  427.6 126.2 %collective-permute-start.34 = (bf16[1024,1280]{1,0:T(8,128)(2,1)}, bf16[1024,1280]{1,0:T(8,128)(2,1)}, u32[]{:S(2)}, u32[]{:S(2)}) collective-permute-start(bf16[1024,1280]{1,0:T(8,128)(2,1)} %collective-permute-done.33.refs_0_.refs_2_), channel_id=1, source_target_pairs={{0,1},{1,0},{2,3},{3,2},{4,5},{5,4},{6,7},{7,6}} | collective-permute-start | bytes 7864328 | tf_op jit(solution)/shard_map/ppermute | solution.py:429
  460.3 184.2 %collective-permute-start.16 = (f32[1024,640]{1,0:T(8,128)}, f32[1024,640]{1,0:T(8,128)S(1)}, u32[]{:S(2)}, u32[]{:S(2)}) collective-permute-start(f32[1024,640]{1,0:T(8,128)} %get-tuple-element.53), channel_id=1, source_target_pairs={{0,1},{1,0},{2,3},{3,2},{4,5},{5,4},{6,7},{7,6}} | collective-permute-start | bytes 7864328 | tf_op jit(solution)/shard_map/ppermute | solution.py:429
  526.3 122.3 %collective-permute-start.27 = (f32[1024,640]{1,0:T(8,128)}, f32[1024,640]{1,0:T(8,128)}, u32[]{:S(2)}, u32[]{:S(2)}) collective-permute-start(f32[1024,640]{1,0:T(8,128)} %get-tuple-element.70), channel_id=1, source_target_pairs={{0,1},{1,0},{2,3},{3,2},{4,5},{5,4},{6,7},{7,6}} | collective-permute-start | bytes 7864328 | tf_op jit(solution)/shard_map/ppermute | solution.py:429
  553.8 56.7 %collective-permute-start.38 = (f32[2,1280]{1,0:T(2,128)S(1)}, f32[2,1280]{1,0:T(2,128)S(1)}, u32[]{:S(2)}, u32[]{:S(2)}) collective-permute-start(f32[2,1280]{1,0:T(2,128)S(1)} %pad_maximum_fusion.2), channel_id=1, source_target_pairs={{0,4},{4,0},{1,5},{5,1},{2,6},{6,2},{3,7},{7,3}} | collective-permute-start | bytes 30728 | tf_op jit(solution)/shard_map/ppermute | solution.py:426
  644.5 170.7 %collective-permute-start.15 = (f32[1024,640]{1,0:T(8,128)}, f32[1024,640]{1,0:T(8,128)}, u32[]{:S(2)}, u32[]{:S(2)}) collective-permute-start(f32[1024,640]{1,0:T(8,128)} %get-tuple-element.52), channel_id=1, source_target_pairs={{0,1},{1,0},{2,3},{3,2},{4,5},{5,4},{6,7},{7,6}} | collective-permute-start | bytes 7864328 | tf_op jit(solution)/shard_map/ppermute | solution.py:429
  648.6 63.1 %collective-permute-start.21 = (f32[1024,640]{1,0:T(8,128)}, f32[1024,640]{1,0:T(8,128)}, u32[]{:S(2)}, u32[]{:S(2)}) collective-permute-start(f32[1024,640]{1,0:T(8,128)} %get-tuple-element.58), channel_id=1, source_target_pairs={{0,1},{1,0},{2,3},{3,2},{4,5},{5,4},{6,7},{7,6}} | collective-permute-start | bytes 7864328 | tf_op jit(solution)/shard_map/ppermute | solution.py:429
  653.1 112.4 %collective-permute-start.26 = (f32[1024,640]{1,0:T(8,128)}, f32[1024,640]{1,0:T(8,128)}, u32[]{:S(2)}, u32[]{:S(2)}) collective-permute-start(f32[1024,640]{1,0:T(8,128)} %get-tuple-element.69), channel_id=1, source_target_pairs={{0,1},{1,0},{2,3},{3,2},{4,5},{5,4},{6,7},{7,6}} | collective-permute-start | bytes 7864328 | tf_op jit(solution)/shard_map/ppermute | solution.py:429
  656.9 108.6 %collective-permute-start.23 = (f32[1024,640]{1,0:T(8,128)}, f32[1024,640]{1,0:T(8,128)S(1)}, u32[]{:S(2)}, u32[]{:S(2)}) collective-permute-start(f32[1024,640]{1,0:T(8,128)} %get-tuple-element.66), channel_id=1, source_target_pairs={{0,1},{1,0},{2,3},{3,2},{4,5},{5,4},{6,7},{7,6}} | collective-permute-start | bytes 7864328 | tf_op jit(solution)/shard_map/ppermute | solution.py:429
  684.3 82.8 %collective-permute-start.28 = (f32[1024,640]{1,0:T(8,128)}, f32[1024,640]{1,0:T(8,128)}, u32[]{:S(2)}, u32[]{:S(2)}) collective-permute-start(f32[1024,640]{1,0:T(8,128)} %slice_add_fusion), channel_id=1, source_target_pairs={{0,2},{2,0},{1,3},{3,1},{4,6},{6,4},{5,7},{7,5}} | collective-permute-start | bytes 7864328 | tf_op jit(solution)/shard_map/ppermute | solution.py:423
  711.7 88.9 %collective-permute-start.25 = (f32[1024,640]{1,0:T(8,128)}, f32[1024,640]{1,0:T(8,128)}, u32[]{:S(2)}, u32[]{:S(2)}) collective-permute-start(f32[1024,640]{1,0:T(8,128)} %slice_add_fusion.1), channel_id=1, source_target_pairs={{0,2},{2,0},{1,3},{3,1},{4,6},{6,4},{5,7},{7,5}} | collective-permute-start | bytes 7864328 | tf_op jit(solution)/shard_map/ppermute | solution.py:423
  765.6 91.2 %collective-permute-start.17 = (f32[1024,640]{1,0:T(8,128)}, f32[1024,640]{1,0:T(8,128)}, u32[]{:S(2)}, u32[]{:S(2)}) collective-permute-start(f32[1024,640]{1,0:T(8,128)} %slice_add_fusion.3), channel_id=1, source_target_pairs={{0,2},{2,0},{1,3},{3,1},{4,6},{6,4},{5,7},{7,5}} | collective-permute-start | bytes 7864328 | tf_op jit(solution)/shard_map/ppermute | solution.py:423
  767.1 145.4 %collective-permute-start.22 = (f32[1024,640]{1,0:T(8,128)}, f32[1024,640]{1,0:T(8,128)}, u32[]{:S(2)}, u32[]{:S(2)}) collective-permute-start(f32[1024,640]{1,0:T(8,128)} %slice_add_fusion.2), channel_id=1, source_target_pairs={{0,2},{2,0},{1,3},{3,1},{4,6},{6,4},{5,7},{7,5}} | collective-permute-start | bytes 7864328 | tf_op jit(solution)/shard_map/ppermute | solution.py:423
  800.6 123.6 %collective-permute-start.37 = (bf16[640,2560]{1,0:T(8,128)(2,1)}, bf16[640,2560]{1,0:T(8,128)(2,1)}, u32[]{:S(2)}, u32[]{:S(2)}) collective-permute-start(bf16[640,2560]{1,0:T(8,128)(2,1)} %get-tuple-element.81), channel_id=1, source_target_pairs={{0,1},{1,0},{2,3},{3,2},{4,5},{5,4},{6,7},{7,6}} | collective-permute-start | bytes 9830408 | tf_op jit(solution)/shard_map/ppermute | solution.py:429
  815.2 114.4 %collective-permute-start.40 = (bf16[1280,1280]{1,0:T(8,128)(2,1)}, bf16[1280,1280]{1,0:T(8,128)(2,1)S(1)}, u32[]{:S(2)}, u32[]{:S(2)}) collective-permute-start(bf16[1280,1280]{1,0:T(8,128)(2,1)} %get-tuple-element.89), channel_id=1, source_target_pairs={{0,1},{1,0},{2,3},{3,2},{4,5},{5,4},{6,7},{7,6}} | collective-permute-start | bytes 9830408 | tf_op jit(solution)/shard_map/ppermute | solution.py:429
  815.5 103.6 %collective-permute-start.41 = (f32[1280]{0:T(1024)S(1)}, f32[1280]{0:T(1024)S(1)}, u32[]{:S(2)}, u32[]{:S(2)}) collective-permute-start(f32[1280]{0:T(1024)S(1)} %get-tuple-element.110), channel_id=1, source_target_pairs={{0,2},{2,0},{1,3},{3,1},{4,6},{6,4},{5,7},{7,5}} | collective-permute-start | bytes 15368 | tf_op jit(solution)/shard_map/ppermute | solution.py:423
  856.8 62.7 %collective-permute-start.43 = (f32[2,1280]{1,0:T(2,128)S(1)}, f32[2,1280]{1,0:T(2,128)S(1)}, u32[]{:S(2)}, u32[]{:S(2)}) collective-permute-start(f32[2,1280]{1,0:T(2,128)S(1)} %pad_maximum_fusion.3), channel_id=1, source_target_pairs={{0,2},{2,0},{1,3},{3,1},{4,6},{6,4},{5,7},{7,5}} | collective-permute-start | bytes 30728 | tf_op jit(solution)/shard_map/ppermute | solution.py:423
  (40 other events, 1119.0 us)

commit v3 on v2

--- a/solution.py
+++ b/solution.py
@@ -148,7 +148,7 @@
     q = w_up.shape[0]
     dm = 4 * q
     ng = len(groups)
-    has_c, has_d = "c" in mode, "d" in mode
+    has_c, has_d = "c" in mode, mode in ("d", "r")
     weights = [w_up, w_down]
     for _, p1, p2, _ in groups:
         weights += (list(p1) if has_c else []) + (list(p2) if has_d else [])
@@ -188,25 +188,23 @@
             arrive(g)
             w1 = bufs.pop(0) if has_c else None
             w2 = bufs.pop(0) if has_d else None
-            s_in = tin.pop(0) if not has_c else None
+            extra = tin.pop(0) if mode in ("d", "ce") else None
             h_out = tout.pop(0) if has_c and groups[g][3] else None
             x_out = tout.pop(0)
             for n0 in range(0, fe, CH_ACT):
                 sl = slice(n0, n0 + CH_ACT)
                 if has_c:
                     c = mm(side(u, v), w1[:, sl]) + cr[g][:, sl]
-                    h, s = gelu_both(c)
+                    h, p = gelu_both(c)
                     if h_out is not None:
                         h_out[:, sl] = h.astype(bf16)
                 else:
-                    s = s_in[:, sl]
-                if has_d:
-                    p = mmt(side(gu, gv), w2[sl, :]) * s
-                    x_out[:, sl] = p.astype(bf16)
-                    if with_sums:
-                        sr[g][:, sl] += jnp.sum(p, axis=0, keepdims=True)
-                else:
-                    x_out[:, sl] = s
+                    p = mmt(side(gu, gv), w2[sl, :])
+                if extra is not None:
+                    p = p * extra[:, sl]
+                x_out[:, sl] = p.astype(x_out.dtype)
+                if with_sums:
+                    sr[g][:, sl] += jnp.sum(p, axis=0, keepdims=True)
 
     scratch = []
     for _ in range(ng):
@@ -215,7 +213,7 @@
     outs = []
     for g in range(ng):
         outs += [(fe, bf16)] if has_c and groups[g][3] else []
-        outs += [(fe, bf16)] if has_d else [(fe, f32)]
+        outs += [(fe, bf16)] if mode in ("d", "ce") else [(fe, f32)]
     n = blocks[0][0].shape[0]
     flops = 2 * n * len(blocks) * dm * fe * ng * (int(has_c) + int(has_d))
     res = tiled_call((load, step), idx, blocks, slopes, weights, [b.reshape(1, fe) for b in biases] if has_c else [],
@@ -440,8 +438,8 @@
         fe = w_up.shape[1] // 4
         row_width = dh_ * dep_size
 
-        def cols(rr, kk):
-            return lax.dynamic_slice_in_dim(w_up, (rr * 2 + kk) * fe, fe, axis=1)
+        def cols(w, rr, kk):
+            return lax.dynamic_slice_in_dim(w, (rr * 2 + kk) * fe, fe, axis=1)
 
         def rows(kk):
             return lax.dynamic_slice_in_dim(w_down, kk * fe, fe, axis=0)
@@ -450,7 +448,9 @@
             return lax.dynamic_slice_in_dim(b_up, (rr * 2 + k) * fe, fe, axis=0).astype(f32)
 
         gx = px(y_grad)
-        own_o, own_n, snd_o, snd_n = cols(r, k), cols(1 - r, k), cols(r, 1 - k), cols(1 - r, 1 - k)
+        own_n = cols(w_up, 1 - r, k)
+        w_rest, own_n = lax.optimization_barrier((w_up, own_n))
+        own_o, snd_o, snd_n = cols(w_rest, r, k), cols(w_rest, r, 1 - k), cols(w_rest, 1 - r, 1 - k)
         w1o = (pd(snd_o), py(own_n), pyd(snd_n))
         w1n = (pd(snd_n), py(own_o), pyd(snd_o))
         rk, rk2 = rows(k), rows(1 - k)
@@ -490,7 +490,8 @@
 
         A0, A1, A2, A3 = [whole(p) for p in A]
 
-        h_o, d_o, sum_o = act("cd", [A[0] + G[0], A[1] + G[1]], [], [go], [bo], True)
+        dh_o, = act("r", [G[0], G[1]], [], [go], [], False)
+        h_o, d_o, sum_o = act("ce", [A[0], A[1]], [dh_o], [go], [bo], True)
         h_n, s_n = act("c", [A[0], A[1]], [], [gn], [bn], False)
         two_o, two_g = [(d_o, 0), (d_o, 1)], [[(G[0][p], 0), (G[1][p], 0)] for p in range(2)]
         dw2 = grad([[(h_o, 0)], [(h_o, 1)]], two_g, [None, None], f32, False)
@@ -540,10 +541,9 @@
         gains = jnp.stack([jnp.sum(norm_grad * x_hat, axis=0), jnp.sum(norm_grad, axis=0)])
 
         dw1n, = grad([A0, A1], [[(d_n, 0), (d_n, 1)]], [None], f32, True)
-        fy = act("d", [G[2]], [syo, syn], [go, gn], [], False)
-        fz = act("d", [G[3]], [szo, szn], [go, gn], [], False)
+        far = act("d", [G[2] + (syo, syn), G[3] + (szo, szn)], [], [go, gn], [], False)
         far_g = [[(G[2][p], 0), (G[3][p], 0)] for p in range(2)]
-        w_up_grad, send1 = final_grad_call(idx, n, [A2, A3], [[(fy[g], 0), (fz[g], 0)] for g in range(2)], [dw1o, dw1n], True)
+        w_up_grad, send1 = final_grad_call(idx, n, [A2, A3], [[(far[g], 0), (far[g], 1)] for g in range(2)], [dw1o, dw1n], True)
         w_down_grad, send2 = final_grad_call(idx, n, [[(hy, 0)], [(hz, 0)]], far_g, dw2, False)
         got1, got2 = pd(send1), pd(send2)
         for g, rr in enumerate((r, 1 - r)):
@@ -551,8 +551,9 @@
         w_down_grad = lax.dynamic_update_slice_in_dim(w_down_grad, got2, (1 - k) * fe, axis=0)
 
         def both(v):
-            v = v + px(v)
-            return v + py(v)
+            near, far = px(v), py(v)
+            cross = lax.ppermute(v, ("row", "col"), CROSS)
+            return (v + near) + (far + cross)
 
         b_down_grad = both(jnp.sum(y_grad.astype(f32), axis=0))
         gain_sums = both(gains)

time: 937 us -> 928 us (level)
  waiting for transfers between devices: 423 us -> 410 us
    ppermute x4, waiting for transfers between devices: 129 us -> 157 us  [pyd(): return lax.ppermute(v, ('row', 'dep'), CROSS)]
    ppermute x9, waiting for transfers between devices: 156 us -> 132 us  [px(): return lax.ppermute(v, 'col', SWAP)]
    ppermute x10, waiting for transfers between devices: 137 us -> 119 us  [py(): return lax.ppermute(v, 'row', SWAP)]
  transfers between devices with their start and end apart: 45 -> 47, of which waited for: 12 -> 14; matrix products, arithmetic and copies ran while one was open for 7% -> 8% of each run, Pallas kernels for 42% -> 43%
where the time goes in v3:
time: 928 us; the launch traced here: 916 us
  waiting for transfers between devices  410 us (44%)
  Pallas kernels  393 us (42%)
  other arithmetic  45.7 us (5%)
  starting transfers between devices  33.6 us (4%)
  local copies, waits for them, and re-layouts  28.1 us (3%)
    pallas_call x11, Pallas kernels, tiled_call(): return call(idx, *ins)  293 us
    ppermute x4, waiting for transfers between devices, pyd(): return lax.ppermute(v, ('row', 'dep'), CROSS)  157 us
    ppermute x9, waiting for transfers between devices, px(): return lax.ppermute(v, 'col', SWAP)  132 us
    ppermute x10, waiting for transfers between devices, py(): return lax.ppermute(v, 'row', SWAP)  119 us
    pallas_call x3, Pallas kernels, grad_call(): pl.pallas_call(kernel, out_shape=[jax.ShapeDtypeStruct((m, fe), out_dtype...  50.8 us
    pallas_call x2, Pallas kernels, final_grad_call(): pl.pallas_call(kernel, out_shape=outs, grid_spec=pltpu.PrefetchScalarGrid...  49.1 us
  transfers between devices with their start and end apart: 47, of which 14 were waited for; matrix products, arithmetic and copies ran while one was open for 8% of the time, Pallas kernels for 43%

profile of v3, /device:TPU:0, one launch (start us, length us, event | category | flops | bytes accessed | tf_op | source)
XLA Modules:
  0.0 916.4 jit_solution(7308671121142951465)
XLA Ops:
  6.7 4.9 constant_dynamic-slice_fusion.4
  23.6 27.0 %collective-permute-done.8.refs_8_.refs_3_.refs_5_ = bf16[640,1280]{1,0:T(8,128)(2,1)} collective-permute-done((bf16[640,1280]{1,0:T(8,128)(2,1)}, bf16[640,1280]{1,0:T(8,128)(2,1)}, u32[]{:S(2)}, u32[]{:S(2)}) %collective-permute-start.8) | collective-permute-done | bytes 1638432 | tf_op jit(solution)/shard_map/ppermute | solution.py:424
  50.6 34.1 %collective-permute-done.9.refs_9_.refs_4_.refs_6_ = bf16[640,1280]{1,0:T(8,128)(2,1)} collective-permute-done((bf16[640,1280]{1,0:T(8,128)(2,1)}, bf16[640,1280]{1,0:T(8,128)(2,1)}, u32[]{:S(2)}, u32[]{:S(2)}) %collective-permute-start.9) | collective-permute-done | bytes 1638432 | tf_op jit(solution)/shard_map/ppermute | solution.py:430
  85.8 31.5 %collective-permute-done.1.refs_2_ = bf16[1024,1280]{1,0:T(8,128)(2,1)S(1)} collective-permute-done((bf16[1024,1280]{1,0:T(8,128)(2,1)}, bf16[1024,1280]{1,0:T(8,128)(2,1)S(1)}, u32[]{:S(2)}, u32[]{:S(2)}) %collective-permute-start.1) | collective-permute-done | bytes 2621472 | tf_op jit(solution)/shard_map/ppermute | solution.py:421
  119.9 5.7 constant_dynamic-slice_fusion
  129.4 22.3 %shard_map.143.refs_4_ = f32[2048,1280]{1,0:T(8,128)} custom-call(s32[2]{0:T(128)} %pad_add_fusion.idx_ref, bf16[1024,1280]{1,0:T(8,128)(2,1)} %refs_2_.7, bf16[1024,1280]{1,0:T(8,128)(2,1)} %collective-permute-done.3.refs_1_.refs_4_, bf16[1024,1280]{1,0:T(8,128)(2,1)} %collective-permute-done.4.refs_2_.refs_3_, ...), custom_call_target="tpu_custom_call" | custom-call | flops 13421772800 | bytes 16777216 | tf_op jit(solution)/shard_map/pallas_call | solution.py:135
  153.8 28.1 %shard_map.144 = (bf16[2048,1280]{1,0:T(8,128)(2,1)}, bf16[2048,1280]{1,0:T(8,128)(2,1)}, f32[1,1280]{1,0:T(1,128)}) custom-call(s32[2]{0:T(128)} %pad_add_fusion.idx_ref, bf16[1024,1280]{1,0:T(8,128)(2,1)} %fusion.8.refs_0_, bf16[1024,1280]{1,0:T(8,128)(2,1)} %collective-permute-done.refs_1_, bf16[1024,1280]{1,0:T(8,128)(2,1)} %copy-done.4, ...), custom_call_target="tpu_custom_call" | custom-call | flops 13421772800 | bytes 16777216 | tf_op jit(solution)/shard_map/pallas_call | solution.py:135
  181.9 17.8 %collective-permute-done.11.refs_7_.refs_11_.refs_8_ = bf16[640,1280]{1,0:T(8,128)(2,1)} collective-permute-done((bf16[640,1280]{1,0:T(8,128)(2,1)}, bf16[640,1280]{1,0:T(8,128)(2,1)}, u32[]{:S(2)}, u32[]{:S(2)}) %collective-permute-start.11) | collective-permute-done | bytes 1638432 | tf_op jit(solution)/shard_map/ppermute | solution.py:424
  201.5 33.3 %collective-permute-done.13.refs_4_.refs_13_.refs_11_ = bf16[1280,640]{1,0:T(8,128)(2,1)} collective-permute-done((bf16[1280,640]{1,0:T(8,128)(2,1)}, bf16[1280,640]{1,0:T(8,128)(2,1)}, u32[]{:S(2)}, u32[]{:S(2)}) %collective-permute-start.13) | collective-permute-done | bytes 1638432 | tf_op jit(solution)/shard_map/ppermute | solution.py:424
  235.3 22.1 %shard_map.149 = (f32[2048,640]{1,0:T(8,128)}, f32[2048,640]{1,0:T(8,128)}, f32[2048,640]{1,0:T(8,128)}, f32[2048,640]{1,0:T(8,128)}) custom-call(s32[2]{0:T(128)} %pad_add_fusion.idx_ref, bf16[2048,1280]{1,0:T(8,128)(2,1)} %get-tuple-element.62.refs_0_.refs_4_.refs_5_, bf16[640,5120]{1,0:T(8,128)(2,1)} %refs_8_.1, ...), custom_call_target="tpu_custom_call" | custom-call | flops 13421772800 | bytes 16777216 | tf_op jit(solution)/shard_map/pallas_call | solution.py:135
  257.4 27.2 %shard_map.145 = (bf16[2048,1280]{1,0:T(8,128)(2,1)}, f32[2048,1280]{1,0:T(8,128)}) custom-call(s32[2]{0:T(128)} %pad_add_fusion.idx_ref, bf16[1024,1280]{1,0:T(8,128)(2,1)} %fusion.8.refs_0_, bf16[1024,1280]{1,0:T(8,128)(2,1)} %collective-permute-done.refs_1_, bf16[1024,1280]{1,0:T(8,128)(2,1)} %copy-done.4, ...), custom_call_target="tpu_custom_call" | custom-call | flops 13421772800 | bytes 16777216 | tf_op jit(solution)/shard_map/pallas_call | solution.py:135
  284.6 6.4 collective-permute-done.29.refs_0_
  291.0 90.6 %collective-permute-done.14.refs_5_.refs_15_.refs_13_ = bf16[1280,640]{1,0:T(8,128)(2,1)} collective-permute-done((bf16[1280,640]{1,0:T(8,128)(2,1)}, bf16[1280,640]{1,0:T(8,128)(2,1)}, u32[]{:S(2)}, u32[]{:S(2)}) %collective-permute-start.14) | collective-permute-done | bytes 1638432 | tf_op jit(solution)/shard_map/ppermute | solution.py:430
  383.0 34.3 %collective-permute-done.18.refs_3_.refs_14_.refs_12_ = bf16[1280,640]{1,0:T(8,128)(2,1)} collective-permute-done((bf16[1280,640]{1,0:T(8,128)(2,1)S(1)}, bf16[1280,640]{1,0:T(8,128)(2,1)}, u32[]{:S(2)}, u32[]{:S(2)}) %collective-permute-start.18) | collective-permute-done | bytes 1638432 | tf_op jit(solution)/shard_map/ppermute | solution.py:424
  419.2 32.5 %collective-permute-done.19.refs_4_.refs_16_.refs_14_ = bf16[1280,640]{1,0:T(8,128)(2,1)} collective-permute-done((bf16[1280,640]{1,0:T(8,128)(2,1)S(1)}, bf16[1280,640]{1,0:T(8,128)(2,1)}, u32[]{:S(2)}, u32[]{:S(2)}) %collective-permute-start.19) | collective-permute-done | bytes 1638432 | tf_op jit(solution)/shard_map/ppermute | solution.py:430
  451.7 43.1 %shard_map.150 = (bf16[2048,1280]{1,0:T(8,128)(2,1)}, f32[2048,640]{1,0:T(8,128)}, f32[2048,640]{1,0:T(8,128)}, f32[1024,640]{1,0:T(8,128)}, f32[1024,640]{1,0:T...) custom-call(s32[2]{0:T(128)} %pad_add_fusion.idx_ref, bf16[1024,1280]{1,0:T(8,128)(2,1)} %refs_2_.7, ...), custom_call_target="tpu_custom_call" | custom-call | flops 26843545600 | bytes 16777216 | tf_op jit(solution)/shard_map/pallas_call | solution.py:135
  496.2 22.4 %shard_map.157 = (f32[1280,1280]{1,0:T(8,128)}, f32[1280,1280]{1,0:T(8,128)}) custom-call(s32[2]{0:T(128)} %pad_add_fusion.idx_ref, bf16[2048,1280]{1,0:T(8,128)(2,1)} %get-tuple-element.51.refs_0_.refs_1_, bf16[2048,1280]{1,0:T(8,128)(2,1)} %get-tuple-element.51.refs_0_.refs_1_, bf16[1024,1280]{1,0:T(8,128)(2,1)} %refs_2_.7, ...), custom_call_target="tpu_custom_call" | custom-call | flops 13421772800 | bytes 16777216 | tf_op jit(solution)/shard_map/pallas_call | solution.py:335
  518.5 22.0 %shard_map.146 = (f32[2048,640]{1,0:T(8,128)}, f32[1024,640]{1,0:T(8,128)}, f32[1024,640]{1,0:T(8,128)}) custom-call(s32[2]{0:T(128)} %pad_add_fusion.idx_ref, bf16[2048,1280]{1,0:T(8,128)(2,1)} %get-tuple-element.51.refs_0_.refs_1_, bf16[2048,1280]{1,0:T(8,128)(2,1)} %get-tuple-element.52.refs_1_.refs_0_, bf16[2560,1280]{1,0:T(8,128)(2,1)} %refs_9_.3, ...), custom_call_target="tpu_custom_call" | custom-call | flops 13421772800 | bytes 16777216 | tf_op jit(solution)/shard_map/pallas_call | solution.py:135
  542.3 27.2 %shard_map.151 = (bf16[1024,1280]{1,0:T(8,128)(2,1)}, f32[1024,1280]{1,0:T(8,128)}, f32[1024,1280]{1,0:T(8,128)}) custom-call(s32[2]{0:T(128)} %pad_add_fusion.idx_ref, bf16[1024,1280]{1,0:T(8,128)(2,1)} %collective-permute-done.29.refs_0_, bf16[1024,1280]{1,0:T(8,128)(2,1)} %collective-permute-done.30.refs_1_, bf16[640,5120]{1,0:T(8,128)(2,1)} %refs_8_.1, ...), custom_call_target="tpu_custom_call" | custom-call | flops 13421772800 | bytes 16777216 | tf_op jit(solution)/shard_map/pallas_call | solution.py:135
  569.5 15.2 %shard_map.147 = (f32[2048,640]{1,0:T(8,128)}, f32[2048,640]{1,0:T(8,128)}) custom-call(s32[2]{0:T(128)} %pad_add_fusion.idx_ref, bf16[2048,1280]{1,0:T(8,128)(2,1)} %get-tuple-element.51.refs_0_.refs_1_, bf16[2560,1280]{1,0:T(8,128)(2,1)} %refs_9_.3, bf16[1280,1280]{1,0:T(8,128)(2,1)} %collective-permute-done.6.refs_6_.refs_3_.refs_2_.refs_10_), custom_call_target="tpu_custom_call" | custom-call | flops 6710886400 | bytes 16777216 | tf_op jit(solution)/shard_map/pallas_call | solution.py:135
  585.3 14.3 %shard_map.154.refs_8_ = f32[1280,1280]{1,0:T(8,128)} custom-call(s32[2]{0:T(128)} %pad_add_fusion.idx_ref, bf16[1024,1280]{1,0:T(8,128)(2,1)} %fusion.8.refs_0_, bf16[1024,1280]{1,0:T(8,128)(2,1)} %collective-permute-done.refs_1_, bf16[1024,1280]{1,0:T(8,128)(2,1)} %copy-done.4, bf16[1024,1280]{1,0:T(8,128)(2,1)} %collective-permute-done.2.refs_3_, ...), custom_call_target="tpu_custom_call" | custom-call | flops 6710886400 | bytes 16777216 | tf_op jit(solution)/shard_map/pallas_call | solution.py:335
  600.1 14.1 %shard_map.155.refs_9_ = f32[1280,1280]{1,0:T(8,128)} custom-call(s32[2]{0:T(128)} %pad_add_fusion.idx_ref, bf16[1024,1280]{1,0:T(8,128)(2,1)} %fusion.8.refs_0_, bf16[1024,1280]{1,0:T(8,128)(2,1)} %collective-permute-done.refs_1_, bf16[1024,1280]{1,0:T(8,128)(2,1)} %copy-done.4, bf16[1024,1280]{1,0:T(8,128)(2,1)} %collective-permute-done.2.refs_3_, ...), custom_call_target="tpu_custom_call" | custom-call | flops 6710886400 | bytes 16777216 | tf_op jit(solution)/shard_map/pallas_call | solution.py:335
  614.3 17.1 %shard_map.148 = (f32[2048,640]{1,0:T(8,128)}, f32[1024,640]{1,0:T(8,128)}, f32[1024,640]{1,0:T(8,128)}) custom-call(s32[2]{0:T(128)} %pad_add_fusion.idx_ref, bf16[2048,1280]{1,0:T(8,128)(2,1)} %get-tuple-element.52.refs_1_.refs_0_, f32[2048,640]{1,0:T(8,128)} %get-tuple-element.56.refs_1_, f32[2048,640]{1,0:T(8,128)} %get-tuple-element.57.refs_2_, ...), custom_call_target="tpu_custom_call" | custom-call | flops 6710886400 | bytes 16777216 | tf_op jit(solution)/shard_map/pallas_call | solution.py:135
  636.7 27.4 %shard_map.152 = (bf16[1024,1280]{1,0:T(8,128)(2,1)}, f32[1024,1280]{1,0:T(8,128)}, f32[1024,1280]{1,0:T(8,128)}) custom-call(s32[2]{0:T(128)} %pad_add_fusion.idx_ref, bf16[1024,1280]{1,0:T(8,128)(2,1)} %collective-permute-done.31.refs_0_.refs_2_, bf16[1024,1280]{1,0:T(8,128)(2,1)} %collective-permute-done.32.refs_1_.refs_3_, bf16[640,5120]{1,0:T(8,128)(2,1)} %refs_8_.1, ...), custom_call_target="tpu_custom_call" | custom-call | flops 13421772800 | bytes 16777216 | tf_op jit(solution)/shard_map/pallas_call | solution.py:135
  666.2 41.4 %shard_map.153 = (bf16[2048,1280]{1,0:T(8,128)(2,1)}, bf16[2048,1280]{1,0:T(8,128)(2,1)}) custom-call(s32[2]{0:T(128)} %pad_add_fusion.idx_ref, bf16[1024,1280]{1,0:T(8,128)(2,1)} %collective-permute-done.33.refs_0_.refs_2_, bf16[1024,1280]{1,0:T(8,128)(2,1)} %collective-permute-done.34.refs_1_.refs_4_, f32[1024,1280]{1,0:T(8,128)} %get-tuple-element.73.refs_2_, ...), custom_call_target="tpu_custom_call" | custom-call | flops 26843545600 | bytes 16777216 | tf_op jit(solution)/shard_map/pallas_call | solution.py:135
  720.5 24.4 %shard_map.156 = (bf16[640,5120]{1,0:T(8,128)(2,1)}, bf16[640,2560]{1,0:T(8,128)(2,1)}) custom-call(s32[2]{0:T(128)} %pad_add_fusion.idx_ref, bf16[1024,1280]{1,0:T(8,128)(2,1)} %collective-permute-done.29.refs_0_, bf16[1024,1280]{1,0:T(8,128)(2,1)} %collective-permute-done.30.refs_1_, bf16[1024,1280]{1,0:T(8,128)(2,1)} %collective-permute-done.31.refs_0_.refs_2_, ...), custom_call_target="tpu_custom_call" | custom-call | flops 13421772800 | bytes 16777216 | tf_op jit(solution)/shard_map/pallas_call | solution.py:401
  747.2 24.6 %shard_map.158 = (bf16[2560,1280]{1,0:T(8,128)(2,1)}, bf16[1280,1280]{1,0:T(8,128)(2,1)}) custom-call(s32[2]{0:T(128)} %pad_add_fusion.idx_ref, bf16[1024,1280]{1,0:T(8,128)(2,1)} %get-tuple-element.84.refs_0_, bf16[1024,1280]{1,0:T(8,128)(2,1)} %get-tuple-element.85.refs_1_, bf16[1024,1280]{1,0:T(8,128)(2,1)} %collective-permute-done.33.refs_0_.refs_2_, ...), custom_call_target="tpu_custom_call" | custom-call | flops 13421772800 | bytes 16777216 | tf_op jit(solution)/shard_map/pallas_call | solution.py:401
  774.7 6.2 collective-permute-done.25
  790.5 5.9 convert_reduce_fusion.1
  796.9 40.2 %collective-permute-done.17 = f32[1024,640]{1,0:T(8,128)} collective-permute-done((f32[1024,640]{1,0:T(8,128)}, f32[1024,640]{1,0:T(8,128)}, u32[]{:S(2)}, u32[]{:S(2)}) %collective-permute-start.17) | collective-permute-done | bytes 2621472 | tf_op jit(solution)/shard_map/ppermute | solution.py:421
  838.5 53.9 %collective-permute-done.22 = f32[1024,640]{1,0:T(8,128)} collective-permute-done((f32[1024,640]{1,0:T(8,128)}, f32[1024,640]{1,0:T(8,128)}, u32[]{:S(2)}, u32[]{:S(2)}) %collective-permute-start.22) | collective-permute-done | bytes 2621472 | tf_op jit(solution)/shard_map/ppermute | solution.py:421
  893.9 6.6 add_convert_fusion.1
  (172 shorter events, 90.9 us)
Async XLA Ops:
  0.6 84.6 %collective-permute-start.4 = (bf16[1024,1280]{1,0:T(8,128)(2,1)}, bf16[1024,1280]{1,0:T(8,128)(2,1)}, u32[]{:S(2)}, u32[]{:S(2)}) collective-permute-start(bf16[1024,1280]{1,0:T(8,128)(2,1)} %refs_2_.7), channel_id=1, source_target_pairs={{0,2},{2,0},{1,3},{3,1},{4,6},{6,4},{5,7},{7,5}} | collective-permute-start | bytes 7864328 | tf_op jit(solution)/shard_map/ppermute | solution.py:421
  13.1 71.6 %collective-permute-start.9 = (bf16[640,1280]{1,0:T(8,128)(2,1)}, bf16[640,1280]{1,0:T(8,128)(2,1)}, u32[]{:S(2)}, u32[]{:S(2)}) collective-permute-start(bf16[640,1280]{1,0:T(8,128)(2,1)} %get-tuple-element.108), channel_id=1, source_target_pairs={{0,5},{1,4},{4,1},{5,0},{2,7},{3,6},{6,3},{7,2}} | collective-permute-start | bytes 4915208 | tf_op jit(solution)/shard_map/ppermute | solution.py:430
  19.4 97.8 %collective-permute-start.1 = (bf16[1024,1280]{1,0:T(8,128)(2,1)}, bf16[1024,1280]{1,0:T(8,128)(2,1)S(1)}, u32[]{:S(2)}, u32[]{:S(2)}) collective-permute-start(bf16[1024,1280]{1,0:T(8,128)(2,1)} %fusion.8.refs_0_), channel_id=1, source_target_pairs={{0,2},{2,0},{1,3},{3,1},{4,6},{6,4},{5,7},{7,5}} | collective-permute-start | bytes 7864328 | tf_op jit(solution)/shard_map/ppermute | solution.py:421
  23.6 103.8 %collective-permute-start.6 = (bf16[1280,1280]{1,0:T(8,128)(2,1)}, bf16[1280,1280]{1,0:T(8,128)(2,1)}, u32[]{:S(2)}, u32[]{:S(2)}) collective-permute-start(bf16[1280,1280]{1,0:T(8,128)(2,1)} %constant_dynamic-slice_fusion.6), channel_id=1, source_target_pairs={{0,1},{1,0},{2,3},{3,2},{4,5},{5,4},{6,7},{7,6}} | collective-permute-start | bytes 9830408 | tf_op jit(solution)/shard_map/ppermute | solution.py:427
  85.3 66.5 %collective-permute-start = (bf16[1024,1280]{1,0:T(8,128)(2,1)}, bf16[1024,1280]{1,0:T(8,128)(2,1)}, u32[]{:S(2)}, u32[]{:S(2)}) collective-permute-start(bf16[1024,1280]{1,0:T(8,128)(2,1)} %fusion.8.refs_0_), channel_id=1, source_target_pairs={{0,1},{1,0},{2,3},{3,2},{4,5},{5,4},{6,7},{7,6}} | collective-permute-start | bytes 7864328 | tf_op jit(solution)/shard_map/ppermute | solution.py:427
  125.6 74.5 %collective-permute-start.12 = (bf16[640,1280]{1,0:T(8,128)(2,1)}, bf16[640,1280]{1,0:T(8,128)(2,1)}, u32[]{:S(2)}, u32[]{:S(2)}) collective-permute-start(bf16[640,1280]{1,0:T(8,128)(2,1)} %get-tuple-element.106), channel_id=1, source_target_pairs={{0,5},{1,4},{4,1},{5,0},{2,7},{3,6},{6,3},{7,2}} | collective-permute-start | bytes 4915208 | tf_op jit(solution)/shard_map/ppermute | solution.py:430
  127.4 72.3 %collective-permute-start.11 = (bf16[640,1280]{1,0:T(8,128)(2,1)}, bf16[640,1280]{1,0:T(8,128)(2,1)}, u32[]{:S(2)}, u32[]{:S(2)}) collective-permute-start(bf16[640,1280]{1,0:T(8,128)(2,1)} %get-tuple-element.107), channel_id=1, source_target_pairs={{0,4},{4,0},{1,5},{5,1},{2,6},{6,2},{3,7},{7,3}} | collective-permute-start | bytes 4915208 | tf_op jit(solution)/shard_map/ppermute | solution.py:424
  127.6 107.2 %collective-permute-start.13 = (bf16[1280,640]{1,0:T(8,128)(2,1)}, bf16[1280,640]{1,0:T(8,128)(2,1)}, u32[]{:S(2)}, u32[]{:S(2)}) collective-permute-start(bf16[1280,640]{1,0:T(8,128)(2,1)} %get-tuple-element.104), channel_id=1, source_target_pairs={{0,4},{4,0},{1,5},{5,1},{2,6},{6,2},{3,7},{7,3}} | collective-permute-start | bytes 4915208 | tf_op jit(solution)/shard_map/ppermute | solution.py:424
  151.7 139.2 %collective-permute-start.29 = (bf16[1024,1280]{1,0:T(8,128)(2,1)}, bf16[1024,1280]{1,0:T(8,128)(2,1)}, u32[]{:S(2)}, u32[]{:S(2)}) collective-permute-start(bf16[1024,1280]{1,0:T(8,128)(2,1)} %fusion.8.refs_0_), channel_id=1, source_target_pairs={{0,4},{4,0},{1,5},{5,1},{2,6},{6,2},{3,7},{7,3}} | collective-permute-start | bytes 7864328 | tf_op jit(solution)/shard_map/ppermute | solution.py:424
  152.0 267.1 %collective-permute-start.33 = (bf16[1024,1280]{1,0:T(8,128)(2,1)}, bf16[1024,1280]{1,0:T(8,128)(2,1)}, u32[]{:S(2)}, u32[]{:S(2)}) collective-permute-start(bf16[1024,1280]{1,0:T(8,128)(2,1)} %refs_2_.7), channel_id=1, source_target_pairs={{0,4},{4,0},{1,5},{5,1},{2,6},{6,2},{3,7},{7,3}} | collective-permute-start | bytes 7864328 | tf_op jit(solution)/shard_map/ppermute | solution.py:424
  199.7 181.9 %collective-permute-start.14 = (bf16[1280,640]{1,0:T(8,128)(2,1)}, bf16[1280,640]{1,0:T(8,128)(2,1)}, u32[]{:S(2)}, u32[]{:S(2)}) collective-permute-start(bf16[1280,640]{1,0:T(8,128)(2,1)} %get-tuple-element.102), channel_id=1, source_target_pairs={{0,5},{1,4},{4,1},{5,0},{2,7},{3,6},{6,3},{7,2}} | collective-permute-start | bytes 4915208 | tf_op jit(solution)/shard_map/ppermute | solution.py:430
  200.1 217.2 %collective-permute-start.18 = (bf16[1280,640]{1,0:T(8,128)(2,1)S(1)}, bf16[1280,640]{1,0:T(8,128)(2,1)}, u32[]{:S(2)}, u32[]{:S(2)}) collective-permute-start(bf16[1280,640]{1,0:T(8,128)(2,1)S(1)} %copy-done.6), channel_id=1, source_target_pairs={{0,4},{4,0},{1,5},{5,1},{2,6},{6,2},{3,7},{7,3}} | collective-permute-start | bytes 4915208 | tf_op jit(solution)/shard_map/ppermute | solution.py:424
  234.8 216.9 %collective-permute-start.19 = (bf16[1280,640]{1,0:T(8,128)(2,1)S(1)}, bf16[1280,640]{1,0:T(8,128)(2,1)}, u32[]{:S(2)}, u32[]{:S(2)}) collective-permute-start(bf16[1280,640]{1,0:T(8,128)(2,1)S(1)} %copy-done.5), channel_id=1, source_target_pairs={{0,5},{1,4},{4,1},{5,0},{2,7},{3,6},{6,3},{7,2}} | collective-permute-start | bytes 4915208 | tf_op jit(solution)/shard_map/ppermute | solution.py:430
  291.0 249.5 %collective-permute-start.30 = (bf16[1024,1280]{1,0:T(8,128)(2,1)}, bf16[1024,1280]{1,0:T(8,128)(2,1)}, u32[]{:S(2)}, u32[]{:S(2)}) collective-permute-start(bf16[1024,1280]{1,0:T(8,128)(2,1)} %collective-permute-done.29.refs_0_), channel_id=1, source_target_pairs={{0,1},{1,0},{2,3},{3,2},{4,5},{5,4},{6,7},{7,6}} | collective-permute-start | bytes 7864328 | tf_op jit(solution)/shard_map/ppermute | solution.py:427
  381.6 160.8 %collective-permute-start.31 = (bf16[1024,1280]{1,0:T(8,128)(2,1)}, bf16[1024,1280]{1,0:T(8,128)(2,1)}, u32[]{:S(2)}, u32[]{:S(2)}) collective-permute-start(bf16[1024,1280]{1,0:T(8,128)(2,1)} %collective-permute-done.29.refs_0_), channel_id=1, source_target_pairs={{0,2},{2,0},{1,3},{3,1},{4,6},{6,4},{5,7},{7,5}} | collective-permute-start | bytes 7864328 | tf_op jit(solution)/shard_map/ppermute | solution.py:421
  417.4 182.2 %collective-permute-start.35 = (bf16[1024,1280]{1,0:T(8,128)(2,1)}, bf16[1024,1280]{1,0:T(8,128)(2,1)}, u32[]{:S(2)}, u32[]{:S(2)}) collective-permute-start(bf16[1024,1280]{1,0:T(8,128)(2,1)} %collective-permute-done.4.refs_2_.refs_3_), channel_id=1, source_target_pairs={{0,4},{4,0},{1,5},{5,1},{2,6},{6,2},{3,7},{7,3}} | collective-permute-start | bytes 7864328 | tf_op jit(solution)/shard_map/ppermute | solution.py:424
  419.1 245.0 %collective-permute-start.34 = (bf16[1024,1280]{1,0:T(8,128)(2,1)}, bf16[1024,1280]{1,0:T(8,128)(2,1)}, u32[]{:S(2)}, u32[]{:S(2)}) collective-permute-start(bf16[1024,1280]{1,0:T(8,128)(2,1)} %collective-permute-done.33.refs_0_.refs_2_), channel_id=1, source_target_pairs={{0,1},{1,0},{2,3},{3,2},{4,5},{5,4},{6,7},{7,6}} | collective-permute-start | bytes 7864328 | tf_op jit(solution)/shard_map/ppermute | solution.py:427
  494.8 137.9 %collective-permute-start.27 = (f32[1024,640]{1,0:T(8,128)}, f32[1024,640]{1,0:T(8,128)S(1)}, u32[]{:S(2)}, u32[]{:S(2)}) collective-permute-start(f32[1024,640]{1,0:T(8,128)} %get-tuple-element.72), channel_id=1, source_target_pairs={{0,1},{1,0},{2,3},{3,2},{4,5},{5,4},{6,7},{7,6}} | collective-permute-start | bytes 7864328 | tf_op jit(solution)/shard_map/ppermute | solution.py:427
  542.3 93.9 %collective-permute-start.32 = (bf16[1024,1280]{1,0:T(8,128)(2,1)}, bf16[1024,1280]{1,0:T(8,128)(2,1)}, u32[]{:S(2)}, u32[]{:S(2)}) collective-permute-start(bf16[1024,1280]{1,0:T(8,128)(2,1)} %collective-permute-done.31.refs_0_.refs_2_), channel_id=1, source_target_pairs={{0,1},{1,0},{2,3},{3,2},{4,5},{5,4},{6,7},{7,6}} | collective-permute-start | bytes 7864328 | tf_op jit(solution)/shard_map/ppermute | solution.py:427
  599.6 64.6 %collective-permute-start.16 = (f32[1024,640]{1,0:T(8,128)}, f32[1024,640]{1,0:T(8,128)}, u32[]{:S(2)}, u32[]{:S(2)}) collective-permute-start(f32[1024,640]{1,0:T(8,128)} %get-tuple-element.55), channel_id=1, source_target_pairs={{0,1},{1,0},{2,3},{3,2},{4,5},{5,4},{6,7},{7,6}} | collective-permute-start | bytes 7864328 | tf_op jit(solution)/shard_map/ppermute | solution.py:427
  599.6 65.1 %collective-permute-start.36 = (bf16[1024,1280]{1,0:T(8,128)(2,1)}, bf16[1024,1280]{1,0:T(8,128)(2,1)}, u32[]{:S(2)}, u32[]{:S(2)}) collective-permute-start(bf16[1024,1280]{1,0:T(8,128)(2,1)} %collective-permute-done.35.refs_4_.refs_3_), channel_id=1, source_target_pairs={{0,1},{1,0},{2,3},{3,2},{4,5},{5,4},{6,7},{7,6}} | collective-permute-start | bytes 7864328 | tf_op jit(solution)/shard_map/ppermute | solution.py:427
  632.7 83.7 %collective-permute-start.21 = (f32[1024,640]{1,0:T(8,128)}, f32[1024,640]{1,0:T(8,128)}, u32[]{:S(2)}, u32[]{:S(2)}) collective-permute-start(f32[1024,640]{1,0:T(8,128)} %get-tuple-element.60), channel_id=1, source_target_pairs={{0,1},{1,0},{2,3},{3,2},{4,5},{5,4},{6,7},{7,6}} | collective-permute-start | bytes 7864328 | tf_op jit(solution)/shard_map/ppermute | solution.py:427
  636.2 108.7 %collective-permute-start.26 = (f32[1024,640]{1,0:T(8,128)}, f32[1024,640]{1,0:T(8,128)S(1)}, u32[]{:S(2)}, u32[]{:S(2)}) collective-permute-start(f32[1024,640]{1,0:T(8,128)} %get-tuple-element.71), channel_id=1, source_target_pairs={{0,1},{1,0},{2,3},{3,2},{4,5},{5,4},{6,7},{7,6}} | collective-permute-start | bytes 7864328 | tf_op jit(solution)/shard_map/ppermute | solution.py:427
  664.2 80.9 %collective-permute-start.23 = (f32[1024,640]{1,0:T(8,128)}, f32[1024,640]{1,0:T(8,128)}, u32[]{:S(2)}, u32[]{:S(2)}) collective-permute-start(f32[1024,640]{1,0:T(8,128)} %get-tuple-element.68), channel_id=1, source_target_pairs={{0,1},{1,0},{2,3},{3,2},{4,5},{5,4},{6,7},{7,6}} | collective-permute-start | bytes 7864328 | tf_op jit(solution)/shard_map/ppermute | solution.py:427
  664.7 81.9 %collective-permute-start.28 = (f32[1024,640]{1,0:T(8,128)}, f32[1024,640]{1,0:T(8,128)}, u32[]{:S(2)}, u32[]{:S(2)}) collective-permute-start(f32[1024,640]{1,0:T(8,128)} %slice_add_fusion), channel_id=1, source_target_pairs={{0,2},{2,0},{1,3},{3,1},{4,6},{6,4},{5,7},{7,5}} | collective-permute-start | bytes 7864328 | tf_op jit(solution)/shard_map/ppermute | solution.py:421
  712.1 84.4 %collective-permute-start.15 = (f32[1024,640]{1,0:T(8,128)}, f32[1024,640]{1,0:T(8,128)}, u32[]{:S(2)}, u32[]{:S(2)}) collective-permute-start(f32[1024,640]{1,0:T(8,128)} %get-tuple-element.54), channel_id=1, source_target_pairs={{0,1},{1,0},{2,3},{3,2},{4,5},{5,4},{6,7},{7,6}} | collective-permute-start | bytes 7864328 | tf_op jit(solution)/shard_map/ppermute | solution.py:427
  745.2 91.9 %collective-permute-start.17 = (f32[1024,640]{1,0:T(8,128)}, f32[1024,640]{1,0:T(8,128)}, u32[]{:S(2)}, u32[]{:S(2)}) collective-permute-start(f32[1024,640]{1,0:T(8,128)} %slice_add_fusion.3), channel_id=1, source_target_pairs={{0,2},{2,0},{1,3},{3,1},{4,6},{6,4},{5,7},{7,5}} | collective-permute-start | bytes 7864328 | tf_op jit(solution)/shard_map/ppermute | solution.py:421
  746.7 145.8 %collective-permute-start.22 = (f32[1024,640]{1,0:T(8,128)}, f32[1024,640]{1,0:T(8,128)}, u32[]{:S(2)}, u32[]{:S(2)}) collective-permute-start(f32[1024,640]{1,0:T(8,128)} %slice_add_fusion.2), channel_id=1, source_target_pairs={{0,2},{2,0},{1,3},{3,1},{4,6},{6,4},{5,7},{7,5}} | collective-permute-start | bytes 7864328 | tf_op jit(solution)/shard_map/ppermute | solution.py:421
  781.0 127.7 %collective-permute-start.37 = (bf16[640,2560]{1,0:T(8,128)(2,1)}, bf16[640,2560]{1,0:T(8,128)(2,1)}, u32[]{:S(2)}, u32[]{:S(2)}) collective-permute-start(bf16[640,2560]{1,0:T(8,128)(2,1)} %get-tuple-element.81), channel_id=1, source_target_pairs={{0,1},{1,0},{2,3},{3,2},{4,5},{5,4},{6,7},{7,6}} | collective-permute-start | bytes 9830408 | tf_op jit(solution)/shard_map/ppermute | solution.py:427
  796.4 117.6 %collective-permute-start.40 = (bf16[1280,1280]{1,0:T(8,128)(2,1)}, bf16[1280,1280]{1,0:T(8,128)(2,1)S(1)}, u32[]{:S(2)}, u32[]{:S(2)}) collective-permute-start(bf16[1280,1280]{1,0:T(8,128)(2,1)} %get-tuple-element.89), channel_id=1, source_target_pairs={{0,1},{1,0},{2,3},{3,2},{4,5},{5,4},{6,7},{7,6}} | collective-permute-start | bytes 9830408 | tf_op jit(solution)/shard_map/ppermute | solution.py:427
  796.7 105.6 %collective-permute-start.42 = (f32[1280]{0:T(1024)S(1)}, f32[1280]{0:T(1024)S(1)}, u32[]{:S(2)}, u32[]{:S(2)}) collective-permute-start(f32[1280]{0:T(1024)S(1)} %get-tuple-element.109), channel_id=1, source_target_pairs={{0,4},{4,0},{1,5},{5,1},{2,6},{6,2},{3,7},{7,3}} | collective-permute-start | bytes 15368 | tf_op jit(solution)/shard_map/ppermute | solution.py:424
  837.1 65.6 %collective-permute-start.43 = (f32[1280]{0:T(1024)S(1)}, f32[1280]{0:T(1024)S(1)}, u32[]{:S(2)}, u32[]{:S(2)}) collective-permute-start(f32[1280]{0:T(1024)S(1)} %get-tuple-element.109), channel_id=1, source_target_pairs={{0,6},{2,4},{4,2},{6,0},{1,7},{3,5},{5,3},{7,1}} | collective-permute-start | bytes 15368 | tf_op jit(solution)/shard_map/ppermute | solution.py:555
  (39 other events, 1154.9 us)
